TPU v7x, 32 devices: a whole 2x2x4 slice. The times are simulated.
32 devices in a mesh: lon: 8 (over y, x, core), lat: 4 (over z).
Axes of the slice: x: 2, y: 2, z: 4, core: 2. Of those that a mesh axis runs over, the one named last changes fastest.
Arguments:
- grid_latent: bfloat16 [4, 8, 1024, 512], P('lat', 'lon'), may hold values from -6 to 6
- mesh_latent: bfloat16 [4, 8, 160, 512], P('lat', 'lon'), may hold values from -6 to 6
- edge_geometry: float32 [4, 8, 4, 2048], P('lat', 'lon'), may hold values from -6 to 6
- senders: int32 [4, 8, 2048], P('lat', 'lon'), may hold values from 0 to 1023
- receivers: int32 [4, 8, 2048], P('lat', 'lon'), may hold values from 0 to 1439, as said below
- w_grid: bfloat16 [512, 512], replicated, may hold values from -0.25 to 0.25
- w_mesh: bfloat16 [512, 512], replicated, may hold values from -0.25 to 0.25
- w_edge: float32 [4, 512], replicated, may hold values from -3 to 3
- edge_bias: float32 [512], replicated, may hold values from -3 to 3
- w_message: bfloat16 [512, 512], replicated, may hold values from -0.25 to 0.25
- w_node: bfloat16 [1024, 512], replicated, may hold values from -0.1875 to 0.1875
- w_output: bfloat16 [512, 512], replicated, may hold values from -0.25 to 0.25
- norm_gain: float32 [512], replicated, may hold values from 0.1 to 1.9
- norm_bias: float32 [512], replicated, may hold values from -3 to 3
Outputs:
- mesh_out: bfloat16 [4, 8, 160, 512], P('lat', 'lon')
Inputs may be any that keep to these rules, and one draw needn't show every extreme that they name: `receivers`: r // 160 is a neighbour slot s from 0 to 8 (latitude offset s // 3 - 1, longitude offset s % 3 - 1); edges of the first band never name latitude offset -1, those of the last band never +1. For s other than 4, with k = s for s < 4 and k = s - 1 otherwise, the row r % 160 lies in k * 16 to k * 16 + 15 for s = 1, 3, 5, 7 and in k * 16 to k * 16 + 3 for s = 0, 2, 6, 8.
All inputs are finite; a program needn't handle non-finite values.
Results may differ from a plain program's by a relative error of at most 0.0095.
Values may be sent and summed in bfloat16 or wider, within the bound.
No kernel may reach another device: no remote copies, remote signals or barrier semaphores. Data moves between devices by JAX's collectives and lax.ppermute only.
A program may use at most 64 MiB of HBM per device.

v0:
```python
import jax
import jax.numpy as jnp
from jax import lax
from jax.sharding import PartitionSpec as P

B_SIDE = 16


border_slots = (0, 1, 2, 3, 5, 6, 7, 8)


def extended(block, sides, width):
    for axis, dim in sides:
        count = lax.axis_size(axis)
        forward = [(i, i + 1) for i in range(count - 1)]
        forward.append((count - 1, 0))
        backward = [(target, source) for source, target in forward]
        low = lax.ppermute(
            lax.slice_in_dim(block, block.shape[dim] - width, None, axis=dim), axis, forward
        )
        high = lax.ppermute(lax.slice_in_dim(block, 0, width, axis=dim), axis, backward)
        block = jnp.concatenate([low, block, high], axis=dim)
    return block


def strip_of(block, slot):
    strip_number = slot if slot < 4 else slot - 1
    return block[strip_number * B_SIDE : (strip_number + 1) * B_SIDE]


def mirrored_cells(block):
    empty = jnp.zeros((B_SIDE, block.shape[1]), block.dtype)
    rows_out = []
    for lat_cell in range(3):
        cells = []
        for lon_cell in range(3):
            slot = (2 - lat_cell) * 3 + (2 - lon_cell)
            cells.append(empty if slot == 4 else strip_of(block, slot))
        rows_out.append(jnp.stack(cells))
    return jnp.stack(rows_out)


def local(
    grid_latent,
    mesh_latent,
    edge_geometry,
    senders,
    receivers,
    w_grid,
    w_mesh,
    w_edge,
    edge_bias,
    w_message,
    w_node,
    w_output,
    norm_gain,
    norm_bias,
):
    grid_rows = grid_latent[0, 0]
    own_mesh = mesh_latent[0, 0]
    geometry = edge_geometry[0, 0]
    sources = senders[0, 0]
    targets = receivers[0, 0]
    mesh_rows = own_mesh.shape[0]
    features = own_mesh.shape[1]
    edge_count = sources.shape[0]
    border_total = 8 * B_SIDE
    padded = extended(mirrored_cells(own_mesh), (("lon", 1), ("lat", 0)), 1)
    received = jnp.concatenate([padded[2 * (s // 3), 2 * (s % 3)] for s in border_slots], axis=0)
    mesh_table = jnp.dot(
        jnp.concatenate([own_mesh, received], axis=0), w_mesh, preferred_element_type=jnp.float32
    )
    slot_number = targets // mesh_rows
    row_number = targets % mesh_rows
    table_index = jnp.where(slot_number == 4, row_number, mesh_rows + row_number)
    slot_total = mesh_rows + border_total
    grid_proj = jnp.dot(grid_rows, w_grid, preferred_element_type=jnp.float32)
    edge_block = min(512, edge_count)
    block_count = edge_count // edge_block
    source_blocks = sources.reshape(block_count, edge_block)
    target_blocks = table_index.reshape(block_count, edge_block)
    geometry_blocks = jnp.transpose(geometry.reshape(4, block_count, edge_block), (1, 0, 2))
    slot_ids = jnp.arange(slot_total, dtype=jnp.int32)

    def add_block(summed, items):
        block_sources, block_targets, block_geometry = items
        grid_term = jnp.take(grid_proj, block_sources, axis=0)
        mesh_term = jnp.take(mesh_table, block_targets, axis=0)
        edge_term = jnp.dot(block_geometry.T, w_edge, precision=lax.Precision.HIGHEST)
        hidden = jax.nn.silu(grid_term + mesh_term + edge_term + edge_bias).astype(jnp.bfloat16)
        message = jnp.dot(hidden, w_message, preferred_element_type=jnp.float32).astype(
            jnp.bfloat16
        )
        target_onehot = (block_targets[:, None] == slot_ids[None, :]).astype(jnp.bfloat16)
        added = lax.dot_general(
            target_onehot, message, (((0,), (0,)), ((), ())), preferred_element_type=jnp.float32
        )
        return (summed + added, None)

    partial_value, _ = lax.scan(
        add_block,
        jnp.zeros((slot_total, features), jnp.float32),
        (source_blocks, target_blocks, geometry_blocks),
    )
    own_part = partial_value[:mesh_rows]
    border_part = partial_value[mesh_rows:]
    empty = jnp.zeros((B_SIDE, features), jnp.float32)
    cells = jnp.stack(
        [
            jnp.stack(
                [empty if a * 3 + b == 4 else strip_of(border_part, a * 3 + b) for b in range(3)]
            )
            for a in range(3)
        ]
    )
    padded = extended(cells.astype(jnp.bfloat16), (("lon", 1), ("lat", 0)), 1).astype(cells.dtype)
    arrived = jnp.concatenate(
        [padded[2 * (2 - s // 3), 2 * (2 - s % 3)] for s in border_slots], axis=0
    )
    arrived = jnp.concatenate(
        [arrived, jnp.zeros((mesh_rows - border_total, features), jnp.float32)], axis=0
    )
    aggregated = own_part + arrived
    node_in = jnp.concatenate([own_mesh, aggregated.astype(jnp.bfloat16)], axis=1)
    node_hidden = jax.nn.silu(jnp.dot(node_in, w_node, preferred_element_type=jnp.float32)).astype(
        jnp.bfloat16
    )
    update = jnp.dot(node_hidden, w_output, preferred_element_type=jnp.float32)
    row_mean = jnp.mean(update, axis=-1, keepdims=True)
    centered = update - row_mean
    row_var = jnp.mean(centered * centered, axis=-1, keepdims=True)
    normed = centered * lax.rsqrt(row_var + 1e-05) * norm_gain + norm_bias
    mesh_out = (own_mesh.astype(jnp.float32) + normed).astype(jnp.bfloat16)
    return mesh_out[None, None]


def solution(mesh):
    return jax.shard_map(
        local,
        mesh=mesh,
        in_specs=(
            P("lat", "lon", None, None),
            P("lat", "lon", None, None),
            P("lat", "lon", None, None),
            P("lat", "lon", None),
            P("lat", "lon", None),
            P(),
            P(),
            P(),
            P(),
            P(),
            P(),
            P(),
            P(),
            P(),
        ),
        out_specs=P("lat", "lon", None, None),
        check_vma=False,
    )
```

profile of v0, /device:TPU:0, one launch (start us, length us, event | category | flops | bytes accessed | tf_op | source)
XLA Modules:
  0.0 78.4 jit_solution(12093431954197767442)
XLA Ops:
  0.0 0.0 copy-start
  0.0 0.9 %slice_bitcast_fusion.31 = (bf16[1,16,512]{2,1,0:T(8,128)(2,1)S(1)}, bf16[1,16,512]{2,1,0:T(8,128)(2,1)S(1)}, bf16[1,16,512]{2,1,0:T(8,128)(2,1)S(1)}, bf16[1,16...) fusion(bf16[1,1,160,512]{3,2,1,0:T(8,128)(2,1)} %param.17), kind=kLoop, calls=%fused_computation.109 | loop fusion | bytes 262144 | tf_op jit(solution)/shard_map/stack | solution.py:39
  0.9 0.1 pad.38.clone
  1.0 0.1 maximum_bitcast_fusion
  1.1 0.5 collective-permute-start
  1.7 2.9 %collective-permute-start.1 = (bf16[3,1,16,512]{3,2,1,0:T(8,128)(2,1)S(1)}, bf16[3,1,16,512]{3,2,1,0:T(8,128)(2,1)S(1)}, u32[]{:S(2)}, u32[]{:S(2)}) collective-permute-start(bf16[3,1,16,512]{3,2,1,0:T(8,128)(2,1)S(1)} %get-tuple-element.149), channel_id=1, source_target_pairs={{4,0},{8,4},{12,8},{16,12},{20,16},{24,20},{28,24},{0,28},{5,1},{9... | collective-permute-start | bytes 147464 | tf_op jit(solution)/shard_map/ppermute | solution.py:21
  4.6 0.9 %constant_dynamic-update-slice_fusion.8 = bf16[288,512]{1,0:T(8,128)(2,1)S(1)} fusion(bf16[1,1,160,512]{3,2,1,0:T(8,128)(2,1)} %param.17), kind=kLoop, calls=%fused_computation.67 | loop fusion | bytes 327680
  5.5 0.0 copy-start.4
  5.5 0.8 divide_reduce_fusion
  6.3 0.0 copy-done
  6.3 0.0 copy-start.2
  6.3 0.0 copy-start.9
  6.3 0.0 copy-start.10
  6.4 3.1 %fusion.7 = f32[1024,512]{1,0:T(8,128)} fusion(bf16[512,512]{1,0:T(8,128)(2,1)} %param.21, bf16[1,1,1024,512]{3,2,1,0:T(8,128)(2,1)S(1)} %copy-done), kind=kOutput, calls=%fused_computation.23 | convolution fusion | flops 536870912 | bytes 3670016 | tf_op jit(solution)/shard_map/dot_general | solution.py:77
  9.5 0.0 copy-done.3
  9.6 0.0 collective-permute-done
  9.6 0.0 collective-permute-done.1
  9.6 2.3 %collective-permute-start.2 = (bf16[1,5,16,512]{3,2,1,0:T(8,128)(2,1)S(1)}, bf16[1,5,16,512]{3,2,1,0:T(8,128)(2,1)S(1)}, u32[]{:S(2)}, u32[]{:S(2)}) collective-permute-start(bf16[1,5,16,512]{3,2,1,0:T(8,128)(2,1)S(1)} %get-tuple-element.137), channel_id=1, source_target_pairs={{0,1},{1,2},{2,3},{3,0},{4,5},{5,6},{6,7},{7,4},{8,9},{9,10},{10,1... | collective-permute-start | bytes 245768 | tf_op jit(solution)/shard_map/ppermute | solution.py:18
  12.0 0.5 broadcast.127
  12.5 0.0 copy-done.4
  12.5 0.6 reduce.13
  13.1 2.1 %collective-permute-start.3 = (bf16[1,5,16,512]{3,2,1,0:T(8,128)(2,1)S(1)}, bf16[1,5,16,512]{3,2,1,0:T(8,128)(2,1)S(1)}, u32[]{:S(2)}, u32[]{:S(2)}) collective-permute-start(bf16[1,5,16,512]{3,2,1,0:T(8,128)(2,1)S(1)} %get-tuple-element.136), channel_id=1, source_target_pairs={{1,0},{2,1},{3,2},{0,3},{5,4},{6,5},{7,6},{4,7},{9,8},{10,9},{11,1... | collective-permute-start | bytes 245768 | tf_op jit(solution)/shard_map/ppermute | solution.py:21
  15.1 1.4 %collective-permute-done.2 = bf16[1,5,16,512]{3,2,1,0:T(8,128)(2,1)S(1)} collective-permute-done((bf16[1,5,16,512]{3,2,1,0:T(8,128)(2,1)S(1)}, bf16[1,5,16,512]{3,2,1,0:T(8,128)(2,1)S(1)}, u32[]{:S(2)}, u32[]{:S(2)}) %collective-permute-start.2) | collective-permute-done | bytes 81952 | tf_op jit(solution)/shard_map/ppermute | solution.py:18
  16.5 1.0 %collective-permute-done.3 = bf16[1,5,16,512]{3,2,1,0:T(8,128)(2,1)S(1)} collective-permute-done((bf16[1,5,16,512]{3,2,1,0:T(8,128)(2,1)S(1)}, bf16[1,5,16,512]{3,2,1,0:T(8,128)(2,1)S(1)}, u32[]{:S(2)}, u32[]{:S(2)}) %collective-permute-start.3) | collective-permute-done | bytes 81952 | tf_op jit(solution)/shard_map/ppermute | solution.py:21
  17.6 0.0 copy-done.2
  17.6 0.3 fusion.27
  17.9 0.0 copy-done.9
  17.9 0.0 copy-done.10
  17.9 45.8 %while.11 = (s32[]{:T(128)}, f32[288,512]{1,0:T(8,128)S(1)}, s32[4,512]{1,0:T(4,128)S(1)}, s32[4,512]{1,0:T(4,128)S(1)}, f32[1024,512]{1,0:T(8,128)}, /*index=5*...) while((s32[]{:T(128)}, f32[288,512]{1,0:T(8,128)S(1)}, ...), condition=%wide.region_1.2_spmd.clone, body=%wide.region_0.1_spmd.clone.sunk | while | flops 435350528 | bytes 9099907 | solution.py:100
  18.0 1.6 %gather_fusion = f32[512,512]{1,0:T(8,128)S(1)} fusion(f32[288,512]{1,0:T(8,128)S(1)} %get-tuple-element.252, s32[1024]{0:T(1024)S(1)} %pad_clamp_fusion.4), kind=kCustom, calls=%fused_computation.1.clone.clone.1 | custom fusion | bytes 2099200 | tf_op jit(solution)/shard_map/while/body/eval_jaxpr/jit(_take)/gather | solution.py:88
  19.6 4.3 %gather_fusion.1 = f32[512,512]{1,0:T(8,128)} fusion(f32[1024,512]{1,0:T(8,128)} %get-tuple-element.251, s32[1024]{0:T(1024)S(1)} %pad_clamp_fusion.5), kind=kCustom, calls=%fused_computation.clone.clone.1 | custom fusion | bytes 2099200 | tf_op jit(solution)/shard_map/while/body/eval_jaxpr/jit(_take)/gather | solution.py:87
  23.9 3.4 %multiply_convert_fusion.3 = bf16[512,512]{1,0:T(8,128)(2,1)} fusion(f32[4,512]{1,0:T(4,128)S(1)} %get-tuple-element.254, f32[512,512]{1,0:T(8,128)S(1)} %gather_fusion, f32[512,512]{1,0:T(8,128)} %gather_fusion.1, f32[512]{0:T(512)S(1)} %get-tuple-element.255, pred[512]{0:T(512)(128)(4,1)S(1)} %compare_and_fusion.4, ...), kind=kOutput, calls=%fused_computation.7.clone.1 | convolution fusion | flops 15204352 | bytes 2641408 | tf_op jit(solution)/shard_map/while/body/eval_jaxpr/dot_general | solution.py:89
  27.4 2.0 %convolution_add_fusion.3 = f32[288,512]{1,0:T(8,128)S(1)} fusion(bf16[512,512]{1,0:T(8,128)(2,1)} %multiply_convert_fusion.3, bf16[512,512]{1,0:T(8,128)(2,1)} %get-tuple-element.256, f32[288,512]{1,0:T(8,128)S(1)} %get-tuple-element.236, s32[512]{0:T(512)S(1)} %bitcast.159, pred[]{:T(512)S(6)} %compare.3), kind=kOutput, calls=%fused_computation.6.clone.1 | convolution fusion | flops 420134912 | bytes 2230273 | tf_op jit(solution)/shard_map/while/body/eval_jaxpr/dot_general | solution.py:95
  29.4 1.6 %gather_fusion = f32[512,512]{1,0:T(8,128)S(1)} fusion(f32[288,512]{1,0:T(8,128)S(1)} %get-tuple-element.252, s32[1024]{0:T(1024)S(1)} %pad_clamp_fusion.4), kind=kCustom, calls=%fused_computation.1.clone.clone.1 | custom fusion | bytes 2099200 | tf_op jit(solution)/shard_map/while/body/eval_jaxpr/jit(_take)/gather | solution.py:88
  31.1 4.3 %gather_fusion.1 = f32[512,512]{1,0:T(8,128)} fusion(f32[1024,512]{1,0:T(8,128)} %get-tuple-element.251, s32[1024]{0:T(1024)S(1)} %pad_clamp_fusion.5), kind=kCustom, calls=%fused_computation.clone.clone.1 | custom fusion | bytes 2099200 | tf_op jit(solution)/shard_map/while/body/eval_jaxpr/jit(_take)/gather | solution.py:87
  35.4 3.4 %multiply_convert_fusion.3 = bf16[512,512]{1,0:T(8,128)(2,1)} fusion(f32[4,512]{1,0:T(4,128)S(1)} %get-tuple-element.254, f32[512,512]{1,0:T(8,128)S(1)} %gather_fusion, f32[512,512]{1,0:T(8,128)} %gather_fusion.1, f32[512]{0:T(512)S(1)} %get-tuple-element.255, pred[512]{0:T(512)(128)(4,1)S(1)} %compare_and_fusion.4, ...), kind=kOutput, calls=%fused_computation.7.clone.1 | convolution fusion | flops 15204352 | bytes 2641408 | tf_op jit(solution)/shard_map/while/body/eval_jaxpr/dot_general | solution.py:89
  38.9 2.0 %convolution_add_fusion.3 = f32[288,512]{1,0:T(8,128)S(1)} fusion(bf16[512,512]{1,0:T(8,128)(2,1)} %multiply_convert_fusion.3, bf16[512,512]{1,0:T(8,128)(2,1)} %get-tuple-element.256, f32[288,512]{1,0:T(8,128)S(1)} %get-tuple-element.236, s32[512]{0:T(512)S(1)} %bitcast.159, pred[]{:T(512)S(6)} %compare.3), kind=kOutput, calls=%fused_computation.6.clone.1 | convolution fusion | flops 420134912 | bytes 2230273 | tf_op jit(solution)/shard_map/while/body/eval_jaxpr/dot_general | solution.py:95
  40.9 1.6 %gather_fusion = f32[512,512]{1,0:T(8,128)S(1)} fusion(f32[288,512]{1,0:T(8,128)S(1)} %get-tuple-element.252, s32[1024]{0:T(1024)S(1)} %pad_clamp_fusion.4), kind=kCustom, calls=%fused_computation.1.clone.clone.1 | custom fusion | bytes 2099200 | tf_op jit(solution)/shard_map/while/body/eval_jaxpr/jit(_take)/gather | solution.py:88
  42.5 4.3 %gather_fusion.1 = f32[512,512]{1,0:T(8,128)} fusion(f32[1024,512]{1,0:T(8,128)} %get-tuple-element.251, s32[1024]{0:T(1024)S(1)} %pad_clamp_fusion.5), kind=kCustom, calls=%fused_computation.clone.clone.1 | custom fusion | bytes 2099200 | tf_op jit(solution)/shard_map/while/body/eval_jaxpr/jit(_take)/gather | solution.py:87
  46.9 3.4 %multiply_convert_fusion.3 = bf16[512,512]{1,0:T(8,128)(2,1)} fusion(f32[4,512]{1,0:T(4,128)S(1)} %get-tuple-element.254, f32[512,512]{1,0:T(8,128)S(1)} %gather_fusion, f32[512,512]{1,0:T(8,128)} %gather_fusion.1, f32[512]{0:T(512)S(1)} %get-tuple-element.255, pred[512]{0:T(512)(128)(4,1)S(1)} %compare_and_fusion.4, ...), kind=kOutput, calls=%fused_computation.7.clone.1 | convolution fusion | flops 15204352 | bytes 2641408 | tf_op jit(solution)/shard_map/while/body/eval_jaxpr/dot_general | solution.py:89
  50.3 2.0 %convolution_add_fusion.3 = f32[288,512]{1,0:T(8,128)S(1)} fusion(bf16[512,512]{1,0:T(8,128)(2,1)} %multiply_convert_fusion.3, bf16[512,512]{1,0:T(8,128)(2,1)} %get-tuple-element.256, f32[288,512]{1,0:T(8,128)S(1)} %get-tuple-element.236, s32[512]{0:T(512)S(1)} %bitcast.159, pred[]{:T(512)S(6)} %compare.3), kind=kOutput, calls=%fused_computation.6.clone.1 | convolution fusion | flops 420134912 | bytes 2230273 | tf_op jit(solution)/shard_map/while/body/eval_jaxpr/dot_general | solution.py:95
  52.3 1.6 %gather_fusion = f32[512,512]{1,0:T(8,128)S(1)} fusion(f32[288,512]{1,0:T(8,128)S(1)} %get-tuple-element.252, s32[1024]{0:T(1024)S(1)} %pad_clamp_fusion.4), kind=kCustom, calls=%fused_computation.1.clone.clone.1 | custom fusion | bytes 2099200 | tf_op jit(solution)/shard_map/while/body/eval_jaxpr/jit(_take)/gather | solution.py:88
  54.0 4.3 %gather_fusion.1 = f32[512,512]{1,0:T(8,128)} fusion(f32[1024,512]{1,0:T(8,128)} %get-tuple-element.251, s32[1024]{0:T(1024)S(1)} %pad_clamp_fusion.5), kind=kCustom, calls=%fused_computation.clone.clone.1 | custom fusion | bytes 2099200 | tf_op jit(solution)/shard_map/while/body/eval_jaxpr/jit(_take)/gather | solution.py:87
  58.3 3.4 %multiply_convert_fusion.3 = bf16[512,512]{1,0:T(8,128)(2,1)} fusion(f32[4,512]{1,0:T(4,128)S(1)} %get-tuple-element.254, f32[512,512]{1,0:T(8,128)S(1)} %gather_fusion, f32[512,512]{1,0:T(8,128)} %gather_fusion.1, f32[512]{0:T(512)S(1)} %get-tuple-element.255, pred[512]{0:T(512)(128)(4,1)S(1)} %compare_and_fusion.4, ...), kind=kOutput, calls=%fused_computation.7.clone.1 | convolution fusion | flops 15204352 | bytes 2641408 | tf_op jit(solution)/shard_map/while/body/eval_jaxpr/dot_general | solution.py:89
  61.8 2.0 %convolution_add_fusion.3 = f32[288,512]{1,0:T(8,128)S(1)} fusion(bf16[512,512]{1,0:T(8,128)(2,1)} %multiply_convert_fusion.3, bf16[512,512]{1,0:T(8,128)(2,1)} %get-tuple-element.256, f32[288,512]{1,0:T(8,128)S(1)} %get-tuple-element.236, s32[512]{0:T(512)S(1)} %bitcast.159, pred[]{:T(512)S(6)} %compare.3), kind=kOutput, calls=%fused_computation.6.clone.1 | convolution fusion | flops 420134912 | bytes 2230273 | tf_op jit(solution)/shard_map/while/body/eval_jaxpr/dot_general | solution.py:95
  63.8 0.0 copy-start.1
  63.8 0.0 copy-start.7
  63.8 0.0 copy-start.8
  63.9 0.1 maximum_bitcast_fusion.4
  64.0 0.1 collective-permute-start.4
  64.1 2.6 %collective-permute-start.5 = (bf16[3,1,16,512]{3,2,1,0:T(8,128)(2,1)S(1)}, bf16[3,1,16,512]{3,2,1,0:T(8,128)(2,1)S(1)}, u32[]{:S(2)}, u32[]{:S(2)}) collective-permute-start(bf16[3,1,16,512]{3,2,1,0:T(8,128)(2,1)S(1)} %get-tuple-element.147), channel_id=1, source_target_pairs={{4,0},{8,4},{12,8},{16,12},{20,16},{24,20},{28,24},{0,28},{5,1},{9... | collective-permute-start | bytes 147464 | tf_op jit(solution)/shard_map/ppermute | solution.py:21
  66.7 1.8 %collective-permute-done.4 = bf16[3,1,16,512]{3,2,1,0:T(8,128)(2,1)S(1)} collective-permute-done((bf16[3,1,16,512]{3,2,1,0:T(8,128)(2,1)S(1)}, bf16[3,1,16,512]{3,2,1,0:T(8,128)(2,1)S(1)}, u32[]{:S(2)}, u32[]{:S(2)}) %collective-permute-start.4) | collective-permute-done | bytes 49184 | tf_op jit(solution)/shard_map/ppermute | solution.py:18
  68.5 0.0 collective-permute-done.5
  68.5 1.6 %collective-permute-start.6 = (bf16[1,5,16,512]{3,2,1,0:T(8,128)(2,1)S(1)}, bf16[1,5,16,512]{3,2,1,0:T(8,128)(2,1)S(1)}, u32[]{:S(2)}, u32[]{:S(2)}) collective-permute-start(bf16[1,5,16,512]{3,2,1,0:T(8,128)(2,1)S(1)} %get-tuple-element.134), channel_id=1, source_target_pairs={{0,1},{1,2},{2,3},{3,0},{4,5},{5,6},{6,7},{7,4},{8,9},{9,10},{10,1... | collective-permute-start | bytes 245768 | tf_op jit(solution)/shard_map/ppermute | solution.py:18
  70.1 2.3 %collective-permute-start.7 = (bf16[1,5,16,512]{3,2,1,0:T(8,128)(2,1)S(1)}, bf16[1,5,16,512]{3,2,1,0:T(8,128)(2,1)S(1)}, u32[]{:S(2)}, u32[]{:S(2)}) collective-permute-start(bf16[1,5,16,512]{3,2,1,0:T(8,128)(2,1)S(1)} %get-tuple-element.135), channel_id=1, source_target_pairs={{1,0},{2,1},{3,2},{0,3},{5,4},{6,5},{7,6},{4,7},{9,8},{10,9},{11,1... | collective-permute-start | bytes 245768 | tf_op jit(solution)/shard_map/ppermute | solution.py:21
  72.4 3.2 %collective-permute-done.6 = bf16[1,5,16,512]{3,2,1,0:T(8,128)(2,1)S(1)} collective-permute-done((bf16[1,5,16,512]{3,2,1,0:T(8,128)(2,1)S(1)}, bf16[1,5,16,512]{3,2,1,0:T(8,128)(2,1)S(1)}, u32[]{:S(2)}, u32[]{:S(2)}) %collective-permute-start.6) | collective-permute-done | bytes 81952 | tf_op jit(solution)/shard_map/ppermute | solution.py:18
  75.7 0.6 collective-permute-done.7
  76.3 0.1 maximum_convert_fusion
  76.5 0.1 add_convert_fusion.1
  76.6 0.0 copy-start.5
  76.6 0.0 copy-start.6
  76.6 0.7 fusion.24
  77.3 0.2 multiply_reduce_fusion
  77.6 0.8 %fusion.18 = bf16[1,1,160,512]{3,2,1,0:T(8,128)(2,1)} fusion(f32[160,512]{1,0:T(8,128)S(1)} %get-tuple-element.151, f32[512]{0:T(512)S(1)} %copy-done.5, f32[512]{0:T(512)S(1)} %copy-done.6, f32[160]{0:T(256)S(1)} %add_rsqrt_fusion, f32[160]{0:T(256)S(1)} %broadcast_multiply_fusion, bf16[1,1,160,512]{3,2,1,0:T(8,128)(2,1)S(1)} %copy-done.1), kind=kLoop, calls=%fused_computation.35 | loop fusion | flops 573440 | bytes 660736 | tf_op jit(solution)/shard_map/broadcast_in_dim | solution.py:134
  (61 shorter events, 0.5 us)
Async XLA Ops:
  0.0 6.3 %copy-start = (bf16[1,1,1024,512]{3,2,1,0:T(8,128)(2,1)S(1)}, bf16[1,1,1024,512]{3,2,1,0:T(8,128)(2,1)}, u32[]{:S(2)}) copy-start(bf16[1,1,1024,512]{3,2,1,0:T(8,128)(2,1)} %param.16) | copy-start | bytes 3145732
  1.1 8.4 %copy-start.3 = (s32[1,1,2048]{2,1,0:T(1,128)S(1)}, s32[1,1,2048]{2,1,0:T(1,128)}, u32[]{:S(2)}) copy-start(s32[1,1,2048]{2,1,0:T(1,128)} %param.20) | copy-start | bytes 24580
  1.1 8.5 %collective-permute-start = (bf16[3,1,16,512]{3,2,1,0:T(8,128)(2,1)S(1)}, bf16[3,1,16,512]{3,2,1,0:T(8,128)(2,1)S(1)}, u32[]{:S(2)}, u32[]{:S(2)}) collective-permute-start(bf16[3,1,16,512]{3,2,1,0:T(8,128)(2,1)S(1)} %get-tuple-element.148), channel_id=1, source_target_pairs={{0,4},{4,8},{8,12},{12,16},{16,20},{20,24},{24,28},{28,0},{1,5},{5... | collective-permute-start | bytes 147464 | tf_op jit(solution)/shard_map/ppermute | solution.py:18
  1.7 7.9 %collective-permute-start.1 = (bf16[3,1,16,512]{3,2,1,0:T(8,128)(2,1)S(1)}, bf16[3,1,16,512]{3,2,1,0:T(8,128)(2,1)S(1)}, u32[]{:S(2)}, u32[]{:S(2)}) collective-permute-start(bf16[3,1,16,512]{3,2,1,0:T(8,128)(2,1)S(1)} %get-tuple-element.149), channel_id=1, source_target_pairs={{4,0},{8,4},{12,8},{16,12},{20,16},{24,20},{28,24},{0,28},{5,1},{9... | collective-permute-start | bytes 147464 | tf_op jit(solution)/shard_map/ppermute | solution.py:21
  5.5 6.9 %copy-start.4 = (s32[1,1,2048]{2,1,0:T(1,128)S(1)}, s32[1,1,2048]{2,1,0:T(1,128)}, u32[]{:S(2)}) copy-start(s32[1,1,2048]{2,1,0:T(1,128)} %param.19) | copy-start | bytes 24580
  6.3 11.2 %copy-start.2 = (bf16[512,512]{1,0:T(8,128)(2,1)S(1)}, bf16[512,512]{1,0:T(8,128)(2,1)}, u32[]{:S(2)}) copy-start(bf16[512,512]{1,0:T(8,128)(2,1)} %param.22) | copy-start | bytes 1572868
  6.3 11.6 %copy-start.9 = (f32[4,512]{1,0:T(4,128)S(1)}, f32[4,512]{1,0:T(4,128)}, u32[]{:S(2)}) copy-start(f32[4,512]{1,0:T(4,128)} %param.23) | copy-start | bytes 24580
  6.3 11.6 %copy-start.10 = (f32[512]{0:T(512)S(1)}, f32[512]{0:T(512)}, u32[]{:S(2)}) copy-start(f32[512]{0:T(512)} %param.24) | copy-start | bytes 6148
  9.6 6.9 %collective-permute-start.2 = (bf16[1,5,16,512]{3,2,1,0:T(8,128)(2,1)S(1)}, bf16[1,5,16,512]{3,2,1,0:T(8,128)(2,1)S(1)}, u32[]{:S(2)}, u32[]{:S(2)}) collective-permute-start(bf16[1,5,16,512]{3,2,1,0:T(8,128)(2,1)S(1)} %get-tuple-element.137), channel_id=1, source_target_pairs={{0,1},{1,2},{2,3},{3,0},{4,5},{5,6},{6,7},{7,4},{8,9},{9,10},{10,1... | collective-permute-start | bytes 245768 | tf_op jit(solution)/shard_map/ppermute | solution.py:18
  13.1 4.5 %collective-permute-start.3 = (bf16[1,5,16,512]{3,2,1,0:T(8,128)(2,1)S(1)}, bf16[1,5,16,512]{3,2,1,0:T(8,128)(2,1)S(1)}, u32[]{:S(2)}, u32[]{:S(2)}) collective-permute-start(bf16[1,5,16,512]{3,2,1,0:T(8,128)(2,1)S(1)} %get-tuple-element.136), channel_id=1, source_target_pairs={{1,0},{2,1},{3,2},{0,3},{5,4},{6,5},{7,6},{4,7},{9,8},{10,9},{11,1... | collective-permute-start | bytes 245768 | tf_op jit(solution)/shard_map/ppermute | solution.py:21
  63.8 12.8 %copy-start.1 = (bf16[1,1,160,512]{3,2,1,0:T(8,128)(2,1)S(1)}, bf16[1,1,160,512]{3,2,1,0:T(8,128)(2,1)}, u32[]{:S(2)}) copy-start(bf16[1,1,160,512]{3,2,1,0:T(8,128)(2,1)} %param.17) | copy-start | bytes 491524
  63.8 12.8 %copy-start.7 = (bf16[1024,512]{1,0:T(8,128)(2,1)S(1)}, bf16[1024,512]{1,0:T(8,128)(2,1)}, u32[]{:S(2)}) copy-start(bf16[1024,512]{1,0:T(8,128)(2,1)} %param.26) | copy-start | bytes 3145732
  63.8 12.8 %copy-start.8 = (bf16[512,512]{1,0:T(8,128)(2,1)S(1)}, bf16[512,512]{1,0:T(8,128)(2,1)}, u32[]{:S(2)}) copy-start(bf16[512,512]{1,0:T(8,128)(2,1)} %param.27) | copy-start | bytes 1572868
  64.0 4.5 %collective-permute-start.4 = (bf16[3,1,16,512]{3,2,1,0:T(8,128)(2,1)S(1)}, bf16[3,1,16,512]{3,2,1,0:T(8,128)(2,1)S(1)}, u32[]{:S(2)}, u32[]{:S(2)}) collective-permute-start(bf16[3,1,16,512]{3,2,1,0:T(8,128)(2,1)S(1)} %get-tuple-element.146), channel_id=1, source_target_pairs={{0,4},{4,8},{8,12},{12,16},{16,20},{20,24},{24,28},{28,0},{1,5},{5... | collective-permute-start | bytes 147464 | tf_op jit(solution)/shard_map/ppermute | solution.py:18
  64.1 4.4 %collective-permute-start.5 = (bf16[3,1,16,512]{3,2,1,0:T(8,128)(2,1)S(1)}, bf16[3,1,16,512]{3,2,1,0:T(8,128)(2,1)S(1)}, u32[]{:S(2)}, u32[]{:S(2)}) collective-permute-start(bf16[3,1,16,512]{3,2,1,0:T(8,128)(2,1)S(1)} %get-tuple-element.147), channel_id=1, source_target_pairs={{4,0},{8,4},{12,8},{16,12},{20,16},{24,20},{28,24},{0,28},{5,1},{9... | collective-permute-start | bytes 147464 | tf_op jit(solution)/shard_map/ppermute | solution.py:21
  68.5 7.2 %collective-permute-start.6 = (bf16[1,5,16,512]{3,2,1,0:T(8,128)(2,1)S(1)}, bf16[1,5,16,512]{3,2,1,0:T(8,128)(2,1)S(1)}, u32[]{:S(2)}, u32[]{:S(2)}) collective-permute-start(bf16[1,5,16,512]{3,2,1,0:T(8,128)(2,1)S(1)} %get-tuple-element.134), channel_id=1, source_target_pairs={{0,1},{1,2},{2,3},{3,0},{4,5},{5,6},{6,7},{7,4},{8,9},{9,10},{10,1... | collective-permute-start | bytes 245768 | tf_op jit(solution)/shard_map/ppermute | solution.py:18
  70.1 6.2 %collective-permute-start.7 = (bf16[1,5,16,512]{3,2,1,0:T(8,128)(2,1)S(1)}, bf16[1,5,16,512]{3,2,1,0:T(8,128)(2,1)S(1)}, u32[]{:S(2)}, u32[]{:S(2)}) collective-permute-start(bf16[1,5,16,512]{3,2,1,0:T(8,128)(2,1)S(1)} %get-tuple-element.135), channel_id=1, source_target_pairs={{1,0},{2,1},{3,2},{0,3},{5,4},{6,5},{7,6},{4,7},{9,8},{10,9},{11,1... | collective-permute-start | bytes 245768 | tf_op jit(solution)/shard_map/ppermute | solution.py:21
  76.6 1.0 %copy-start.5 = (f32[512]{0:T(512)S(1)}, f32[512]{0:T(512)}, u32[]{:S(2)}) copy-start(f32[512]{0:T(512)} %param.29) | copy-start | bytes 6148
  76.6 1.0 %copy-start.6 = (f32[512]{0:T(512)S(1)}, f32[512]{0:T(512)}, u32[]{:S(2)}) copy-start(f32[512]{0:T(512)} %param.28) | copy-start | bytes 6148
where the time goes:
time: 78.9 us; the launch traced here: 78.4 us
  local copies, waits for them, and re-layouts  26.4 us (33%)
  matrix products  25.8 us (33%)
  starting transfers between devices  14.5 us (18%)
  waiting for transfers between devices  8.01 us (10%)
  other arithmetic  3.05 us (4%)
    gather x4, local copies, waits for them, and re-layouts, add_block(): grid_term = jnp.take(grid_proj, block_sources, axis=0)  17.3 us
    dot_general x4, matrix products, add_block(): jnp.dot(block_geometry.T, w_edge, precision=lax.Precision.HIGHEST)  13.8 us
    ppermute x4, starting transfers between devices, extended(): lax.ppermute(lax.slice_in_dim(block, 0, width, axis=dim), axis, backward)  9.99 us
    dot_general x4, matrix products, add_block(): lax.dot_general(target_onehot, message, (((0,), (0,)), ((), ())), preferr...  7.88 us
    gather x4, local copies, waits for them, and re-layouts, add_block(): mesh_term = jnp.take(mesh_table, block_targets, axis=0)  6.48 us
    ppermute x4, waiting for transfers between devices, extended(): lax.ppermute(lax.slice_in_dim(block, block.shape[dim] - width, None, axis...  6.36 us
    ppermute x4, starting transfers between devices, extended(): lax.ppermute(lax.slice_in_dim(block, block.shape[dim] - width, None, axis...  4.56 us
    dot_general x1, matrix products, local(): grid_proj = jnp.dot(grid_rows, w_grid, preferred_element_type=jnp.float32)  3.13 us
  transfers between devices with their start and end apart: 8, of which 5 were waited for; matrix products, arithmetic and copies ran while one was open for 8% of the time, Pallas kernels for 0%

commit v1 on v0

v1 whole, which is shorter than its diff:
```python
import functools

import jax
import jax.numpy as jnp
from jax import lax
from jax.experimental import pallas as pl
from jax.experimental.pallas import tpu as pltpu
from jax.sharding import PartitionSpec as P

B_SIDE = 16
B_CORNER = 4
CORNER_ROWS = 8
SEND_ROWS = B_SIDE + 2 * CORNER_ROWS
GEOMETRY_ROWS = 16
side_slots = (5, 3, 1, 7)
corner_slots = (2, 0, 8, 6)
BORDER = len(side_slots) * B_SIDE + len(corner_slots) * B_CORNER

bf16 = jnp.bfloat16
f32 = jnp.float32


def strip_row(slot):
    return (slot if slot < 4 else slot - 1) * B_SIDE


def silu(x):
    half = 0.5 * x
    return half + half * jnp.tanh(half)


def dot(a, b, dims=(((1,), (0,)), ((), ()))):
    return lax.dot_general(a, b, dims, preferred_element_type=f32)


def grid_kernel(senders, grid_rows, w_grid, out, proj, *, block):
    nodes = grid_rows.shape[0]
    proj[...] = dot(grid_rows[...], w_grid[...]).astype(bf16)
    for start in range(0, out.shape[0], block):
        picks = jnp.broadcast_to(senders[:, start : start + block], (128, block)).T
        lane = lax.broadcasted_iota(jnp.int32, (block, 128), 1)
        onehot = jnp.concatenate(
            [(picks - base == lane).astype(f32).astype(bf16) for base in range(0, nodes, 128)],
            axis=1,
        )
        out[start : start + block] = dot(onehot, proj[...])


def edge_kernel(
    grid_term,
    own_mesh,
    from_right,
    from_left,
    from_below,
    from_above,
    targets,
    geometry,
    w_mesh,
    w_edge,
    edge_bias,
    w_message,
    own_sum,
    to_right,
    to_left,
    to_above,
    to_below,
    table,
    factors,
    summed,
    *,
    block,
):
    mesh_rows = own_mesh.shape[0]
    border_end = mesh_rows + BORDER
    received = (from_right, from_left, from_below, from_above)
    table[:mesh_rows] = dot(own_mesh[...], w_mesh[...])
    arrived = dot(jnp.concatenate([ref[...] for ref in received], axis=0), w_mesh[...])
    row = mesh_rows
    for i in range(4):
        table[row : row + B_SIDE] = arrived[i * SEND_ROWS : i * SEND_ROWS + B_SIDE]
        row += B_SIDE
    for i in (2, 3):
        for j in range(2):
            first = i * SEND_ROWS + B_SIDE + j * CORNER_ROWS
            table[row : row + B_CORNER] = arrived[first : first + B_CORNER]
            row += B_CORNER
    w_high = w_edge[...].astype(bf16).astype(f32)
    bias = edge_bias[...]
    bias_high = bias.astype(bf16).astype(f32)
    table[row : row + 4] = w_high
    table[row + 4 : row + 8] = w_edge[...] - w_high
    table[row + 8 : row + 12] = w_high
    table[row + 12 : row + 13] = bias_high
    table[row + 13 : row + 14] = bias - bias_high
    table[row + 14 : row + 16] = jnp.zeros((2, table.shape[1]), f32)
    table_bf16 = table[...].astype(bf16)

    high = geometry[...].astype(bf16).astype(f32)
    factors[0:4] = high
    factors[4:8] = high
    factors[8:12] = geometry[...] - high
    factors[12:14] = jnp.ones((2, factors.shape[1]), f32)
    factors[14:16] = jnp.zeros((2, factors.shape[1]), f32)

    places = {}
    for i, slot in enumerate(side_slots):
        places[slot] = mesh_rows + i * B_SIDE
    for i, slot in enumerate(corner_slots):
        places[slot] = mesh_rows + len(side_slots) * B_SIDE + i * B_CORNER
    named = targets[...]
    shift = jnp.zeros_like(named)
    for slot in range(9):
        base = slot * mesh_rows
        if slot != 4:
            base += strip_row(slot) - places[slot]
        shift = jnp.where(named >= slot * mesh_rows, base, shift)
    index = named - shift

    total = None
    for start in range(0, grid_term.shape[0], block):
        ids = lax.broadcasted_iota(jnp.int32, (border_end, block), 0)
        onehot = (ids == index[:, start : start + block]).astype(f32).astype(bf16)
        picks = jnp.concatenate(
            [onehot, factors[:, start : start + block].astype(bf16)], axis=0
        )
        preact = grid_term[start : start + block] + dot(
            picks, table_bf16, (((0,), (0,)), ((), ()))
        )
        hidden = silu(preact).astype(bf16)
        message = dot(hidden, w_message[...]).astype(bf16)
        added = dot(onehot, message)
        total = added if total is None else total + added
    summed[...] = total
    own_sum[...] = summed[:mesh_rows]
    sent = {}
    for slot in side_slots:
        sent[slot] = summed[places[slot] : places[slot] + B_SIDE]
    pad = jnp.zeros((CORNER_ROWS - B_CORNER, table.shape[1]), f32)
    for slot in corner_slots:
        rows = summed[places[slot] : places[slot] + B_CORNER]
        sent[slot] = jnp.concatenate([rows, pad], axis=0)
    to_right[...] = jnp.concatenate([sent[5], sent[2], sent[8]], axis=0).astype(bf16)
    to_left[...] = jnp.concatenate([sent[3], sent[0], sent[6]], axis=0).astype(bf16)
    to_above[...] = sent[7].astype(bf16)
    to_below[...] = sent[1].astype(bf16)


def node_kernel(
    own_mesh,
    own_sum,
    from_left,
    from_right,
    from_below,
    from_above,
    w_node,
    w_output,
    norm_gain,
    norm_bias,
    out,
    agg,
):
    features = own_mesh.shape[1]
    agg[...] = own_sum[...]
    for ref, slots in ((from_left, (5,)), (from_right, (3,)), (from_below, (7, 8, 6)), (from_above, (1, 2, 0))):
        first = 0
        for slot in slots:
            rows = B_SIDE if slot % 2 else CORNER_ROWS
            place = strip_row(slot)
            agg[place : place + rows] += ref[...].astype(f32)[first : first + rows]
            first += rows
    hidden = dot(own_mesh[...], w_node[:features]) + dot(agg[...].astype(bf16), w_node[features:])
    hidden = silu(hidden).astype(bf16)
    update = dot(hidden, w_output[...])
    mean = jnp.mean(update, axis=-1, keepdims=True)
    centered = update - mean
    var = jnp.mean(centered * centered, axis=-1, keepdims=True)
    normed = centered * lax.rsqrt(var + 1e-05) * norm_gain[...] + norm_bias[...]
    out[...] = (own_mesh[...].astype(f32) + normed).astype(bf16)


def shift_by(block, axis, step, wrap):
    count = lax.axis_size(axis)
    pairs = [(i, (i + step) % count) for i in range(count) if wrap or 0 <= i + step < count]
    return lax.ppermute(block, axis, pairs)


def local(
    grid_latent,
    mesh_latent,
    edge_geometry,
    senders,
    receivers,
    w_grid,
    w_mesh,
    w_edge,
    edge_bias,
    w_message,
    w_node,
    w_output,
    norm_gain,
    norm_bias,
):
    grid_rows = grid_latent[0, 0]
    own_mesh = mesh_latent[0, 0]
    mesh_rows, features = own_mesh.shape
    edges = senders.shape[2]
    block = min(512, edges)
    table_rows = mesh_rows + BORDER + GEOMETRY_ROWS

    def piece(slot, rows):
        return lax.slice_in_dim(own_mesh, strip_row(slot), strip_row(slot) + rows)

    def side(slot):
        return piece(slot, B_SIDE)

    def corner(slot):
        return piece(slot, CORNER_ROWS)

    cat = functools.partial(jnp.concatenate, axis=0)
    from_right = shift_by(cat([side(5), corner(2), corner(8)]), "lon", -1, True)
    from_left = shift_by(cat([side(3), corner(0), corner(6)]), "lon", 1, True)
    mid, end = B_SIDE + CORNER_ROWS, SEND_ROWS
    from_below = shift_by(
        cat([side(1), from_right[B_SIDE:mid], from_left[B_SIDE:mid]]), "lat", 1, False
    )
    from_above = shift_by(
        cat([side(7), from_right[mid:end], from_left[mid:end]]), "lat", -1, False
    )

    grid_term = pl.pallas_call(
        functools.partial(grid_kernel, block=block),
        out_shape=jax.ShapeDtypeStruct((edges, features), f32),
        scratch_shapes=[pltpu.VMEM(grid_rows.shape, bf16)],
        cost_estimate=pl.CostEstimate(flops=6_000_000_000, transcendentals=0, bytes_accessed=6_000_000),
        name="grid_term",
    )(senders[0], grid_rows, w_grid)

    packed = jax.ShapeDtypeStruct((SEND_ROWS, features), bf16)
    strip = jax.ShapeDtypeStruct((B_SIDE, features), bf16)
    own_sum, to_right, to_left, to_above, to_below = pl.pallas_call(
        functools.partial(edge_kernel, block=block),
        out_shape=(jax.ShapeDtypeStruct((mesh_rows, features), f32), packed, packed, strip, strip),
        scratch_shapes=[
            pltpu.VMEM((table_rows, features), f32),
            pltpu.VMEM((GEOMETRY_ROWS, edges), f32),
            pltpu.VMEM((mesh_rows + BORDER, features), f32),
        ],
        name="edge_sums",
    )(
        grid_term,
        own_mesh,
        from_right,
        from_left,
        from_below,
        from_above,
        receivers[0],
        edge_geometry[0, 0],
        w_mesh,
        w_edge,
        edge_bias[None],
        w_message,
    )

    got_left = shift_by(to_right, "lon", 1, True)
    got_right = shift_by(to_left, "lon", -1, True)
    got_below = shift_by(cat([to_above, got_left[mid:end], got_right[mid:end]]), "lat", 1, False)
    got_above = shift_by(
        cat([to_below, got_left[B_SIDE:mid], got_right[B_SIDE:mid]]), "lat", -1, False
    )
    mesh_out = pl.pallas_call(
        node_kernel,
        out_shape=jax.ShapeDtypeStruct(own_mesh.shape, bf16),
        scratch_shapes=[pltpu.VMEM((mesh_rows, features), f32)],
        name="node_update",
    )(
        own_mesh,
        own_sum,
        got_left,
        got_right,
        got_below,
        got_above,
        w_node,
        w_output,
        norm_gain[None],
        norm_bias[None],
    )
    return mesh_out[None, None]


def solution(mesh):
    return jax.shard_map(
        local,
        mesh=mesh,
        in_specs=(
            P("lat", "lon", None, None),
            P("lat", "lon", None, None),
            P("lat", "lon", None, None),
            P("lat", "lon", None),
            P("lat", "lon", None),
            P(),
            P(),
            P(),
            P(),
            P(),
            P(),
            P(),
            P(),
            P(),
        ),
        out_specs=P("lat", "lon", None, None),
        check_vma=False,
    )
```

time: 78.9 us -> 48.4 us (0.61)
  matrix products: 25.8 us -> 0 us
  local copies, waits for them, and re-layouts: 26.4 us -> 2.75 us
  Pallas kernels: 0 us -> 16.1 us
  waiting for transfers between devices: 8.01 us -> 10.6 us
  starting transfers between devices: 14.5 us -> 16.6 us
  other arithmetic: 3.05 us -> 1.48 us
    dot_general x11 -> x0, matrix products: 25.8 us -> none  [the longest x4 13.8 us: add_block(): jnp.dot(block_geometry.T, w_edge, precision=lax.Precision.HIGHEST)]
    gather x8 -> x0, local copies, waits for them, and re-layouts: 23.8 us -> none  [the longest x4 17.3 us: add_block(): grid_term = jnp.take(grid_proj, block_sources, axis=0)]
    pallas_call x0 -> x3, Pallas kernels: none -> 16.1 us  [the longest x1 6.68 us: local(): pl.pallas_call(functools.partial(edge_kernel, block=block), out_shape=(ja...]
    ppermute x8, waiting for transfers between devices: 8.01 us -> 10.6 us  [shift_by(): return lax.ppermute(block, axis, pairs)]
    ppermute x8, starting transfers between devices: 14.5 us -> 16.6 us  [shift_by(): return lax.ppermute(block, axis, pairs)]
    slice x0 -> x6, local copies, waits for them, and re-layouts: none -> 1.53 us  [the longest x2 1.52 us: piece(): return lax.slice_in_dim(own_mesh, strip_row(slot), strip_row(slot) + rows)]
    concatenate x1 -> x6, other arithmetic: 0.03 us -> 1.48 us  [the longest x1 0.73 us: local(): cat([to_above, got_left[mid:end], got_right[mid:end]])]
    another operation x4 -> x0, local copies, waits for them, and re-layouts: 1.03 us -> none  [the longest x2 1.01 us: mirrored_cells(): rows_out.append(jnp.stack(cells))]
  transfers between devices with their start and end apart: 8 -> 8, of which waited for: 5 -> 5; matrix products, arithmetic and copies ran while one was open for 8% -> 2% of each run, Pallas kernels for 0% -> 13%
where the time goes in v1:
time: 48.4 us; the launch traced here: 47.8 us
  starting transfers between devices  16.6 us (34%)
  Pallas kernels  16.1 us (33%)
  waiting for transfers between devices  10.6 us (22%)
  local copies, waits for them, and re-layouts  2.75 us (6%)
  other arithmetic  1.48 us (3%)
    ppermute x8, starting transfers between devices, shift_by(): return lax.ppermute(block, axis, pairs)  16.6 us
    ppermute x8, waiting for transfers between devices, shift_by(): return lax.ppermute(block, axis, pairs)  10.6 us
    pallas_call x1, Pallas kernels, local(): pl.pallas_call(functools.partial(edge_kernel, block=block), out_shape=(ja...  6.68 us
    pallas_call x1, Pallas kernels, local(): pl.pallas_call(functools.partial(grid_kernel, block=block), out_shape=jax...  6.44 us
    pallas_call x1, Pallas kernels, local(): pl.pallas_call(node_kernel, out_shape=jax.ShapeDtypeStruct(own_mesh.shape...  3.02 us
    slice x2, local copies, waits for them, and re-layouts, piece(): return lax.slice_in_dim(own_mesh, strip_row(slot), strip_row(slot) + rows)  1.52 us
    unnamed x16, local copies, waits for them, and re-layouts  1.22 us
  transfers between devices with their start and end apart: 8, of which 5 were waited for; matrix products, arithmetic and copies ran while one was open for 2% of the time, Pallas kernels for 13%

profile of v1, /device:TPU:0, one launch (start us, length us, event | category | flops | bytes accessed | tf_op | source)
XLA Modules:
  0.0 47.8 jit_solution(12642606053999744048)
XLA Ops:
  0.0 0.7 %slice_bitcast_fusion.5 = (bf16[8,512]{1,0:T(8,128)(2,1)S(1)}, bf16[8,512]{1,0:T(8,128)(2,1)S(1)}, bf16[8,512]{1,0:T(8,128)(2,1)S(1)}, bf16[8,512]{1,0:T(8,128)(2,1)S(1)}) fusion(bf16[1,1,160,512]{3,2,1,0:T(8,128)(2,1)} %param.15), kind=kLoop, calls=%fused_computation.11 | loop fusion | bytes 65536 | tf_op jit(solution)/shard_map/slice | solution.py:211
  0.8 0.8 %slice_bitcast_fusion = (bf16[16,512]{1,0:T(8,128)(2,1)S(1)}, bf16[16,512]{1,0:T(8,128)(2,1)S(1)}, bf16[16,512]{1,0:T(8,128)(2,1)S(1)}, bf16[16,512]{1,0:T(8,128)(2,1)S(1)}) fusion(bf16[1,1,160,512]{3,2,1,0:T(8,128)(2,1)} %param.15), kind=kLoop, calls=%fused_computation.6 | loop fusion | bytes 131072 | tf_op jit(solution)/shard_map/slice | solution.py:211
  1.5 3.4 %collective-permute-start = (bf16[32,512]{1,0:T(8,128)(2,1)S(1)}, bf16[32,512]{1,0:T(8,128)(2,1)S(1)}, u32[]{:S(2)}, u32[]{:S(2)}) collective-permute-start(bf16[32,512]{1,0:T(8,128)(2,1)S(1)} %pad_maximum_fusion), channel_id=1, source_target_pairs={{0,28},{4,0},{8,4},{12,8},{16,12},{20,16},{24,20},{28,24},{1,29},{... | collective-permute-start | bytes 98312 | tf_op jit(solution)/shard_map/ppermute | solution.py:184
  4.9 0.0 collective-permute-start.1
  5.0 1.6 %collective-permute-done.from_right = bf16[32,512]{1,0:T(8,128)(2,1)S(1)} collective-permute-done((bf16[32,512]{1,0:T(8,128)(2,1)S(1)}, bf16[32,512]{1,0:T(8,128)(2,1)S(1)}, u32[]{:S(2)}, u32[]{:S(2)}) %collective-permute-start) | collective-permute-done | bytes 32800 | tf_op jit(solution)/shard_map/ppermute | solution.py:184
  6.5 0.0 copy-start
  6.5 2.6 %collective-permute-done.1.from_left = bf16[32,512]{1,0:T(8,128)(2,1)S(1)} collective-permute-done((bf16[32,512]{1,0:T(8,128)(2,1)S(1)}, bf16[32,512]{1,0:T(8,128)(2,1)S(1)}, u32[]{:S(2)}, u32[]{:S(2)}) %collective-permute-start.1) | collective-permute-done | bytes 32800 | tf_op jit(solution)/shard_map/ppermute | solution.py:184
  9.2 0.0 copy-start.1
  9.2 3.5 %collective-permute-start.2 = (bf16[32,512]{1,0:T(8,128)(2,1)S(1)}, bf16[32,512]{1,0:T(8,128)(2,1)S(1)}, u32[]{:S(2)}, u32[]{:S(2)}) collective-permute-start(bf16[32,512]{1,0:T(8,128)(2,1)S(1)} %pad_maximum_fusion.2), channel_id=1, source_target_pairs={{0,1},{1,2},{2,3},{4,5},{5,6},{6,7},{8,9},{9,10},{10,11},{12,13},{... | collective-permute-start | bytes 98312 | tf_op jit(solution)/shard_map/ppermute | solution.py:184
  12.7 1.3 %collective-permute-start.3 = (bf16[32,512]{1,0:T(8,128)(2,1)S(1)}, bf16[32,512]{1,0:T(8,128)(2,1)S(1)}, u32[]{:S(2)}, u32[]{:S(2)}) collective-permute-start(bf16[32,512]{1,0:T(8,128)(2,1)S(1)} %pad_maximum_fusion.3), channel_id=1, source_target_pairs={{1,0},{2,1},{3,2},{5,4},{6,5},{7,6},{9,8},{10,9},{11,10},{13,12},{... | collective-permute-start | bytes 98312 | tf_op jit(solution)/shard_map/ppermute | solution.py:184
  14.0 6.4 %grid_term.1 = f32[2048,512]{1,0:T(8,128)} custom-call(s32[1,2048]{1,0:T(1,128)} %bitcast.33, bf16[1024,512]{1,0:T(8,128)(2,1)} %bitcast.32, bf16[512,512]{1,0:T(8,128)(2,1)} %w_grid.1), custom_call_target="tpu_custom_call" | custom-call | flops 6000000000 | bytes 6000000 | tf_op jit(solution)/shard_map/grid_term/pallas_call | solution.py:230
  20.4 0.0 copy-done
  20.4 0.0 copy-done.1
  20.5 0.0 collective-permute-done.2.from_below
  20.5 0.0 copy-start.4
  20.5 0.0 collective-permute-done.3.from_above
  20.5 0.0 copy-start.6
  20.5 0.6 %copy-done.4 = bf16[32,512]{1,0:T(8,128)(2,1)} copy-done((bf16[32,512]{1,0:T(8,128)(2,1)}, bf16[32,512]{1,0:T(8,128)(2,1)S(1)}, u32[]{:S(2)}) %copy-start.4) | copy-done | bytes 32792
  21.1 0.0 copy-done.6
  21.1 6.7 %edge_sums.1 = (f32[160,512]{1,0:T(8,128)}, bf16[32,512]{1,0:T(8,128)(2,1)}, bf16[32,512]{1,0:T(8,128)(2,1)}, bf16[16,512]{1,0:T(8,128)(2,1)}, bf16[16,512]{1,0:T(8,128)(2,1)}) custom-call(f32[2048,512]{1,0:T(8,128)} %grid_term.1, bf16[160,512]{1,0:T(8,128)(2,1)} %bitcast.25, bf16[32,512]{1,0:T(8,128)(2,1)} %copy-done, bf16[32,512]{1,0:T(8,128)(2,1)} %copy-done.1, ...), custom_call_target="tpu_custom_call" | custom-call | tf_op jit(solution)/shard_map/edge_sums/pallas_call | solution.py:240
  27.8 0.0 collective-permute-start.4
  27.8 2.6 %collective-permute-start.5 = (bf16[32,512]{1,0:T(8,128)(2,1)}, bf16[32,512]{1,0:T(8,128)(2,1)S(1)}, u32[]{:S(2)}, u32[]{:S(2)}) collective-permute-start(bf16[32,512]{1,0:T(8,128)(2,1)} %get-tuple-element.12), channel_id=1, source_target_pairs={{0,28},{4,0},{8,4},{12,8},{16,12},{20,16},{24,20},{28,24},{1,29},{... | collective-permute-start | bytes 98312 | tf_op jit(solution)/shard_map/ppermute | solution.py:184
  30.4 1.8 %collective-permute-done.4.from_left = bf16[32,512]{1,0:T(8,128)(2,1)S(1)} collective-permute-done((bf16[32,512]{1,0:T(8,128)(2,1)}, bf16[32,512]{1,0:T(8,128)(2,1)S(1)}, u32[]{:S(2)}, u32[]{:S(2)}) %collective-permute-start.4) | collective-permute-done | bytes 32800 | tf_op jit(solution)/shard_map/ppermute | solution.py:184
  32.2 0.0 copy-start.2
  32.2 0.1 collective-permute-done.5.from_right
  32.3 0.0 copy-start.3
  32.3 0.7 %pad_maximum_fusion.4 = bf16[32,512]{1,0:T(8,128)(2,1)S(1)} fusion(bf16[8,512]{1,0:T(8,128)(2,1)S(1)} %get-tuple-element.26, bf16[8,512]{1,0:T(8,128)(2,1)S(1)} %get-tuple-element.24, bf16[16,512]{1,0:T(8,128)(2,1)} %get-tuple-element.13), kind=kLoop, calls=%fused_computation.4 | loop fusion | flops 98304 | bytes 65536 | tf_op jit(solution)/shard_map/concatenate | solution.py:266
  33.1 4.5 %collective-permute-start.6 = (bf16[32,512]{1,0:T(8,128)(2,1)S(1)}, bf16[32,512]{1,0:T(8,128)(2,1)S(1)}, u32[]{:S(2)}, u32[]{:S(2)}) collective-permute-start(bf16[32,512]{1,0:T(8,128)(2,1)S(1)} %pad_maximum_fusion.4), channel_id=1, source_target_pairs={{0,1},{1,2},{2,3},{4,5},{5,6},{6,7},{8,9},{9,10},{10,11},{12,13},{... | collective-permute-start | bytes 98312 | tf_op jit(solution)/shard_map/ppermute | solution.py:184
  37.6 0.7 %pad_maximum_fusion.5 = bf16[32,512]{1,0:T(8,128)(2,1)S(1)} fusion(bf16[8,512]{1,0:T(8,128)(2,1)S(1)} %get-tuple-element.25, bf16[8,512]{1,0:T(8,128)(2,1)S(1)} %get-tuple-element.23, bf16[16,512]{1,0:T(8,128)(2,1)} %get-tuple-element.14), kind=kLoop, calls=%fused_computation.5 | loop fusion | flops 98304 | bytes 65536 | tf_op jit(solution)/shard_map/concatenate | solution.py:268
  38.3 1.3 %collective-permute-start.7 = (bf16[32,512]{1,0:T(8,128)(2,1)S(1)}, bf16[32,512]{1,0:T(8,128)(2,1)S(1)}, u32[]{:S(2)}, u32[]{:S(2)}) collective-permute-start(bf16[32,512]{1,0:T(8,128)(2,1)S(1)} %pad_maximum_fusion.5), channel_id=1, source_target_pairs={{1,0},{2,1},{3,2},{5,4},{6,5},{7,6},{9,8},{10,9},{11,10},{13,12},{... | collective-permute-start | bytes 98312 | tf_op jit(solution)/shard_map/ppermute | solution.py:184
  39.6 0.0 collective-permute-done.6.from_below
  39.6 0.0 copy-start.5
  39.6 4.5 %collective-permute-done.7.from_above = bf16[32,512]{1,0:T(8,128)(2,1)S(1)} collective-permute-done((bf16[32,512]{1,0:T(8,128)(2,1)S(1)}, bf16[32,512]{1,0:T(8,128)(2,1)S(1)}, u32[]{:S(2)}, u32[]{:S(2)}) %collective-permute-start.7) | collective-permute-done | bytes 32800 | tf_op jit(solution)/shard_map/ppermute | solution.py:184
  44.1 0.0 copy-start.7
  44.1 0.0 copy-done.2
  44.1 0.0 copy-done.3
  44.1 0.0 copy-done.5
  44.1 0.6 %copy-done.7 = bf16[32,512]{1,0:T(8,128)(2,1)} copy-done((bf16[32,512]{1,0:T(8,128)(2,1)}, bf16[32,512]{1,0:T(8,128)(2,1)S(1)}, u32[]{:S(2)}) %copy-start.7) | copy-done | bytes 32792
  44.7 3.0 %node_update.1 = bf16[160,512]{1,0:T(8,128)(2,1)} custom-call(bf16[160,512]{1,0:T(8,128)(2,1)} %bitcast.26, f32[160,512]{1,0:T(8,128)} %get-tuple-element.10.own_sum, bf16[32,512]{1,0:T(8,128)(2,1)} %copy-done.2, bf16[32,512]{1,0:T(8,128)(2,1)} %copy-done.3, bf16[32,512]{1,0:T(8,128)(2,1)} %copy-done.5, bf16[32,512]{1,0:T(8,128)(2,1)} %copy-done.7, ...), custom_call_target="tpu_custom_call" | custom-call | tf_op jit(solution)/shard_map/node_update/pallas_call | solution.py:270
  (8 shorter events, 0.0 us)
Async XLA Ops:
  1.5 5.0 %collective-permute-start = (bf16[32,512]{1,0:T(8,128)(2,1)S(1)}, bf16[32,512]{1,0:T(8,128)(2,1)S(1)}, u32[]{:S(2)}, u32[]{:S(2)}) collective-permute-start(bf16[32,512]{1,0:T(8,128)(2,1)S(1)} %pad_maximum_fusion), channel_id=1, source_target_pairs={{0,28},{4,0},{8,4},{12,8},{16,12},{20,16},{24,20},{28,24},{1,29},{... | collective-permute-start | bytes 98312 | tf_op jit(solution)/shard_map/ppermute | solution.py:184
  4.9 4.2 %collective-permute-start.1 = (bf16[32,512]{1,0:T(8,128)(2,1)S(1)}, bf16[32,512]{1,0:T(8,128)(2,1)S(1)}, u32[]{:S(2)}, u32[]{:S(2)}) collective-permute-start(bf16[32,512]{1,0:T(8,128)(2,1)S(1)} %pad_maximum_fusion.1), channel_id=1, source_target_pairs={{0,4},{4,8},{8,12},{12,16},{16,20},{20,24},{24,28},{28,0},{1,5},{5... | collective-permute-start | bytes 98312 | tf_op jit(solution)/shard_map/ppermute | solution.py:184
  6.5 13.9 %copy-start = (bf16[32,512]{1,0:T(8,128)(2,1)}, bf16[32,512]{1,0:T(8,128)(2,1)S(1)}, u32[]{:S(2)}) copy-start(bf16[32,512]{1,0:T(8,128)(2,1)S(1)} %collective-permute-done.from_right) | copy-start | bytes 98308
  9.2 11.3 %copy-start.1 = (bf16[32,512]{1,0:T(8,128)(2,1)}, bf16[32,512]{1,0:T(8,128)(2,1)S(1)}, u32[]{:S(2)}) copy-start(bf16[32,512]{1,0:T(8,128)(2,1)S(1)} %collective-permute-done.1.from_left) | copy-start | bytes 98308
  9.2 11.3 %collective-permute-start.2 = (bf16[32,512]{1,0:T(8,128)(2,1)S(1)}, bf16[32,512]{1,0:T(8,128)(2,1)S(1)}, u32[]{:S(2)}, u32[]{:S(2)}) collective-permute-start(bf16[32,512]{1,0:T(8,128)(2,1)S(1)} %pad_maximum_fusion.2), channel_id=1, source_target_pairs={{0,1},{1,2},{2,3},{4,5},{5,6},{6,7},{8,9},{9,10},{10,11},{12,13},{... | collective-permute-start | bytes 98312 | tf_op jit(solution)/shard_map/ppermute | solution.py:184
  12.7 7.8 %collective-permute-start.3 = (bf16[32,512]{1,0:T(8,128)(2,1)S(1)}, bf16[32,512]{1,0:T(8,128)(2,1)S(1)}, u32[]{:S(2)}, u32[]{:S(2)}) collective-permute-start(bf16[32,512]{1,0:T(8,128)(2,1)S(1)} %pad_maximum_fusion.3), channel_id=1, source_target_pairs={{1,0},{2,1},{3,2},{5,4},{6,5},{7,6},{9,8},{10,9},{11,10},{13,12},{... | collective-permute-start | bytes 98312 | tf_op jit(solution)/shard_map/ppermute | solution.py:184
  20.5 0.6 %copy-start.4 = (bf16[32,512]{1,0:T(8,128)(2,1)}, bf16[32,512]{1,0:T(8,128)(2,1)S(1)}, u32[]{:S(2)}) copy-start(bf16[32,512]{1,0:T(8,128)(2,1)S(1)} %collective-permute-done.2.from_below) | copy-start | bytes 98308
  20.5 0.6 %copy-start.6 = (bf16[32,512]{1,0:T(8,128)(2,1)}, bf16[32,512]{1,0:T(8,128)(2,1)S(1)}, u32[]{:S(2)}) copy-start(bf16[32,512]{1,0:T(8,128)(2,1)S(1)} %collective-permute-done.3.from_above) | copy-start | bytes 98308
  27.8 4.4 %collective-permute-start.4 = (bf16[32,512]{1,0:T(8,128)(2,1)}, bf16[32,512]{1,0:T(8,128)(2,1)S(1)}, u32[]{:S(2)}, u32[]{:S(2)}) collective-permute-start(bf16[32,512]{1,0:T(8,128)(2,1)} %get-tuple-element.11), channel_id=1, source_target_pairs={{0,4},{4,8},{8,12},{12,16},{16,20},{20,24},{24,28},{28,0},{1,5},{5... | collective-permute-start | bytes 98312 | tf_op jit(solution)/shard_map/ppermute | solution.py:184
  27.8 4.6 %collective-permute-start.5 = (bf16[32,512]{1,0:T(8,128)(2,1)}, bf16[32,512]{1,0:T(8,128)(2,1)S(1)}, u32[]{:S(2)}, u32[]{:S(2)}) collective-permute-start(bf16[32,512]{1,0:T(8,128)(2,1)} %get-tuple-element.12), channel_id=1, source_target_pairs={{0,28},{4,0},{8,4},{12,8},{16,12},{20,16},{24,20},{28,24},{1,29},{... | collective-permute-start | bytes 98312 | tf_op jit(solution)/shard_map/ppermute | solution.py:184
  32.2 11.9 %copy-start.2 = (bf16[32,512]{1,0:T(8,128)(2,1)}, bf16[32,512]{1,0:T(8,128)(2,1)S(1)}, u32[]{:S(2)}) copy-start(bf16[32,512]{1,0:T(8,128)(2,1)S(1)} %collective-permute-done.4.from_left) | copy-start | bytes 98308
  32.3 11.8 %copy-start.3 = (bf16[32,512]{1,0:T(8,128)(2,1)}, bf16[32,512]{1,0:T(8,128)(2,1)S(1)}, u32[]{:S(2)}) copy-start(bf16[32,512]{1,0:T(8,128)(2,1)S(1)} %collective-permute-done.5.from_right) | copy-start | bytes 98308
  33.1 6.6 %collective-permute-start.6 = (bf16[32,512]{1,0:T(8,128)(2,1)S(1)}, bf16[32,512]{1,0:T(8,128)(2,1)S(1)}, u32[]{:S(2)}, u32[]{:S(2)}) collective-permute-start(bf16[32,512]{1,0:T(8,128)(2,1)S(1)} %pad_maximum_fusion.4), channel_id=1, source_target_pairs={{0,1},{1,2},{2,3},{4,5},{5,6},{6,7},{8,9},{9,10},{10,11},{12,13},{... | collective-permute-start | bytes 98312 | tf_op jit(solution)/shard_map/ppermute | solution.py:184
  38.3 5.8 %collective-permute-start.7 = (bf16[32,512]{1,0:T(8,128)(2,1)S(1)}, bf16[32,512]{1,0:T(8,128)(2,1)S(1)}, u32[]{:S(2)}, u32[]{:S(2)}) collective-permute-start(bf16[32,512]{1,0:T(8,128)(2,1)S(1)} %pad_maximum_fusion.5), channel_id=1, source_target_pairs={{1,0},{2,1},{3,2},{5,4},{6,5},{7,6},{9,8},{10,9},{11,10},{13,12},{... | collective-permute-start | bytes 98312 | tf_op jit(solution)/shard_map/ppermute | solution.py:184
  39.6 4.5 %copy-start.5 = (bf16[32,512]{1,0:T(8,128)(2,1)}, bf16[32,512]{1,0:T(8,128)(2,1)S(1)}, u32[]{:S(2)}) copy-start(bf16[32,512]{1,0:T(8,128)(2,1)S(1)} %collective-permute-done.6.from_below) | copy-start | bytes 98308
  44.1 0.6 %copy-start.7 = (bf16[32,512]{1,0:T(8,128)(2,1)}, bf16[32,512]{1,0:T(8,128)(2,1)S(1)}, u32[]{:S(2)}) copy-start(bf16[32,512]{1,0:T(8,128)(2,1)S(1)} %collective-permute-done.7.from_above) | copy-start | bytes 98308

commit v2 on v1

--- a/solution.py
+++ b/solution.py
@@ -178,10 +178,49 @@
     out[...] = (own_mesh[...].astype(f32) + normed).astype(bf16)
 
 
-def shift_by(block, axis, step, wrap):
+def pack_sides_kernel(own_mesh, to_left, to_right):
+    for out, slots in ((to_left, (5, 2, 8)), (to_right, (3, 0, 6))):
+        pieces = [
+            own_mesh[strip_row(slot) : strip_row(slot) + (B_SIDE if slot % 2 else CORNER_ROWS)]
+            for slot in slots
+        ]
+        out[...] = jnp.concatenate(pieces, axis=0)
+
+
+def pack_bands_kernel(
+    up_side, down_side, from_right, from_left, to_above, to_below, *, up_row, down_row, up_first
+):
+    first, second = B_SIDE, B_SIDE + CORNER_ROWS
+    up, down = (first, second) if up_first else (second, first)
+    for out, side, row, corner in (
+        (to_above, up_side, up_row, up),
+        (to_below, down_side, down_row, down),
+    ):
+        out[:B_SIDE] = side[row : row + B_SIDE]
+        for i, ref in enumerate((from_right, from_left)):
+            place = B_SIDE + i * CORNER_ROWS
+            out[place : place + CORNER_ROWS] = ref[corner : corner + CORNER_ROWS]
+
+
+def on_chip(x):
+    return pltpu.with_memory_space_constraint(x, pltpu.VMEM)
+
+
+def call(kernel, name, outs, args, scratch=(), flops=0):
+    cost = pl.CostEstimate(flops=flops, transcendentals=0, bytes_accessed=0) if flops else None
+    return pl.pallas_call(
+        kernel,
+        out_shape=tuple(pltpu.VMEM(shape, dtype) for shape, dtype in outs),
+        scratch_shapes=list(scratch),
+        cost_estimate=cost,
+        compiler_params=pltpu.CompilerParams(vmem_limit_bytes=24 * 2**20),
+        name=name,
+    )(*(on_chip(x) for x in args))
+
+
+def shift_by(block, axis, step):
     count = lax.axis_size(axis)
-    pairs = [(i, (i + step) % count) for i in range(count) if wrap or 0 <= i + step < count]
-    return lax.ppermute(block, axis, pairs)
+    return lax.ppermute(block, axis, [(i, (i + step) % count) for i in range(count)])
 
 
 def local(
@@ -207,82 +246,83 @@
     block = min(512, edges)
     table_rows = mesh_rows + BORDER + GEOMETRY_ROWS
 
-    def piece(slot, rows):
-        return lax.slice_in_dim(own_mesh, strip_row(slot), strip_row(slot) + rows)
-
-    def side(slot):
-        return piece(slot, B_SIDE)
-
-    def corner(slot):
-        return piece(slot, CORNER_ROWS)
-
-    cat = functools.partial(jnp.concatenate, axis=0)
-    from_right = shift_by(cat([side(5), corner(2), corner(8)]), "lon", -1, True)
-    from_left = shift_by(cat([side(3), corner(0), corner(6)]), "lon", 1, True)
-    mid, end = B_SIDE + CORNER_ROWS, SEND_ROWS
-    from_below = shift_by(
-        cat([side(1), from_right[B_SIDE:mid], from_left[B_SIDE:mid]]), "lat", 1, False
-    )
-    from_above = shift_by(
-        cat([side(7), from_right[mid:end], from_left[mid:end]]), "lat", -1, False
-    )
-
-    grid_term = pl.pallas_call(
+    packed = ((SEND_ROWS, features), bf16)
+    strip = ((B_SIDE, features), bf16)
+
+    to_left, to_right = call(pack_sides_kernel, "pack_sides", (packed, packed), (own_mesh,))
+    from_right = shift_by(to_left, "lon", -1)
+    from_left = shift_by(to_right, "lon", 1)
+    to_above, to_below = call(
+        functools.partial(
+            pack_bands_kernel, up_row=strip_row(1), down_row=strip_row(7), up_first=True
+        ),
+        "pack_bands",
+        (packed, packed),
+        (own_mesh, own_mesh, from_right, from_left),
+    )
+    from_below = shift_by(to_above, "lat", 1)
+    from_above = shift_by(to_below, "lat", -1)
+
+    (grid_term,) = call(
         functools.partial(grid_kernel, block=block),
-        out_shape=jax.ShapeDtypeStruct((edges, features), f32),
-        scratch_shapes=[pltpu.VMEM(grid_rows.shape, bf16)],
-        cost_estimate=pl.CostEstimate(flops=6_000_000_000, transcendentals=0, bytes_accessed=6_000_000),
-        name="grid_term",
-    )(senders[0], grid_rows, w_grid)
-
-    packed = jax.ShapeDtypeStruct((SEND_ROWS, features), bf16)
-    strip = jax.ShapeDtypeStruct((B_SIDE, features), bf16)
-    own_sum, to_right, to_left, to_above, to_below = pl.pallas_call(
+        "grid_term",
+        (((edges, features), f32),),
+        (senders[0], grid_rows, w_grid),
+        [pltpu.VMEM(grid_rows.shape, bf16)],
+        flops=6_000_000_000,
+    )
+    own_sum, to_right, to_left, to_above, to_below = call(
         functools.partial(edge_kernel, block=block),
-        out_shape=(jax.ShapeDtypeStruct((mesh_rows, features), f32), packed, packed, strip, strip),
-        scratch_shapes=[
+        "edge_sums",
+        ((own_mesh.shape, f32), packed, packed, strip, strip),
+        (
+            grid_term,
+            own_mesh,
+            from_right,
+            from_left,
+            from_below,
+            from_above,
+            receivers[0],
+            edge_geometry[0, 0],
+            w_mesh,
+            w_edge,
+            edge_bias[None],
+            w_message,
+        ),
+        [
             pltpu.VMEM((table_rows, features), f32),
             pltpu.VMEM((GEOMETRY_ROWS, edges), f32),
             pltpu.VMEM((mesh_rows + BORDER, features), f32),
         ],
-        name="edge_sums",
-    )(
-        grid_term,
-        own_mesh,
-        from_right,
-        from_left,
-        from_below,
-        from_above,
-        receivers[0],
-        edge_geometry[0, 0],
-        w_mesh,
-        w_edge,
-        edge_bias[None],
-        w_message,
-    )
-
-    got_left = shift_by(to_right, "lon", 1, True)
-    got_right = shift_by(to_left, "lon", -1, True)
-    got_below = shift_by(cat([to_above, got_left[mid:end], got_right[mid:end]]), "lat", 1, False)
-    got_above = shift_by(
-        cat([to_below, got_left[B_SIDE:mid], got_right[B_SIDE:mid]]), "lat", -1, False
-    )
-    mesh_out = pl.pallas_call(
+    )
+
+    got_left = shift_by(to_right, "lon", 1)
+    got_right = shift_by(to_left, "lon", -1)
+    to_above, to_below = call(
+        functools.partial(pack_bands_kernel, up_row=0, down_row=0, up_first=False),
+        "pack_sums",
+        (packed, packed),
+        (to_above, to_below, got_left, got_right),
+    )
+    got_below = shift_by(to_above, "lat", 1)
+    got_above = shift_by(to_below, "lat", -1)
+    (mesh_out,) = call(
         node_kernel,
-        out_shape=jax.ShapeDtypeStruct(own_mesh.shape, bf16),
-        scratch_shapes=[pltpu.VMEM((mesh_rows, features), f32)],
-        name="node_update",
-    )(
-        own_mesh,
-        own_sum,
-        got_left,
-        got_right,
-        got_below,
-        got_above,
-        w_node,
-        w_output,
-        norm_gain[None],
-        norm_bias[None],
+        "node_update",
+        ((own_mesh.shape, bf16),),
+        (
+            own_mesh,
+            own_sum,
+            got_left,
+            got_right,
+            got_below,
+            got_above,
+            w_node,
+            w_output,
+            norm_gain[None],
+            norm_bias[None],
+        ),
+        [pltpu.VMEM((mesh_rows, features), f32)],
     )
     return mesh_out[None, None]
 

time: 48.4 us -> 33.8 us (0.70)
  Pallas kernels: 16.1 us -> 7.18 us
  waiting for transfers between devices: 10.6 us -> 7.73 us
  starting transfers between devices: 16.6 us -> 13.8 us
  local copies, waits for them, and re-layouts: 2.75 us -> 4.6 us
  other arithmetic: 1.48 us -> 0 us
    pallas_call x3 -> x6, Pallas kernels: 16.1 us -> 7.18 us  [call(): pl.pallas_call(kernel, out_shape=tuple((pltpu.VMEM(shape, dtype) for shap...]
    unnamed x16 -> x31, local copies, waits for them, and re-layouts: 1.22 us -> 4.6 us
    ppermute x8, waiting for transfers between devices: 10.6 us -> 7.73 us  [shift_by(): lax.ppermute(block, axis, [(i, (i + step) % count) for i in range(count)])]
    ppermute x8, starting transfers between devices: 16.6 us -> 13.8 us  [shift_by(): lax.ppermute(block, axis, [(i, (i + step) % count) for i in range(count)])]
    slice x6 -> x0, local copies, waits for them, and re-layouts: 1.53 us -> none  [the longest x2 1.52 us: piece(): return lax.slice_in_dim(own_mesh, strip_row(slot), strip_row(slot) + rows)]
    concatenate x6 -> x0, other arithmetic: 1.48 us -> none  [the longest x1 0.73 us: local(): cat([to_above, got_left[mid:end], got_right[mid:end]])]
  transfers between devices with their start and end apart: 8 -> 8, of which waited for: 5 -> 4; matrix products, arithmetic and copies ran while one was open for 2% -> 0% of each run, Pallas kernels for 13% -> 9%
where the time goes in v2:
time: 33.8 us; the launch traced here: 33.5 us
  starting transfers between devices  13.8 us (41%)
  waiting for transfers between devices  7.73 us (23%)
  Pallas kernels  7.18 us (21%)
  local copies, waits for them, and re-layouts  4.6 us (14%)
    ppermute x8, starting transfers between devices, shift_by(): lax.ppermute(block, axis, [(i, (i + step) % count) for i in range(count)])  13.8 us
    ppermute x8, waiting for transfers between devices, shift_by(): lax.ppermute(block, axis, [(i, (i + step) % count) for i in range(count)])  7.73 us
    pallas_call x6, Pallas kernels, call(): pl.pallas_call(kernel, out_shape=tuple((pltpu.VMEM(shape, dtype) for shap...  7.18 us
    unnamed x31, local copies, waits for them, and re-layouts  4.6 us
  transfers between devices with their start and end apart: 8, of which 4 were waited for; matrix products, arithmetic and copies ran while one was open for 0% of the time, Pallas kernels for 9%

profile of v2, /device:TPU:0, one launch (start us, length us, event | category | flops | bytes accessed | tf_op | source)
XLA Modules:
  0.0 33.5 jit_solution(8945987037189081795)
XLA Ops:
  0.0 0.0 copy-start
  0.0 0.9 %copy-done = bf16[1,1,160,512]{3,2,1,0:T(8,128)(2,1)S(1)} copy-done((bf16[1,1,160,512]{3,2,1,0:T(8,128)(2,1)S(1)}, bf16[1,1,160,512]{3,2,1,0:T(8,128)(2,1)}, u32[]{:S(2)}) %copy-start) | copy-done | bytes 163864
  0.9 3.4 %collective-permute-start = (bf16[32,512]{1,0:T(8,128)(2,1)S(1)}, bf16[32,512]{1,0:T(8,128)(2,1)S(1)}, u32[]{:S(2)}, u32[]{:S(2)}) collective-permute-start(bf16[32,512]{1,0:T(8,128)(2,1)S(1)} %get-tuple-element.16), channel_id=1, source_target_pairs={{0,28},{4,0},{8,4},{12,8},{16,12},{20,16},{24,20},{28,24},{1,29},{... | collective-permute-start | bytes 98312 | tf_op jit(solution)/shard_map/ppermute | solution.py:223
  4.3 0.0 collective-permute-start.1
  4.3 1.6 %collective-permute-done.from_right = bf16[32,512]{1,0:T(8,128)(2,1)S(1)} collective-permute-done((bf16[32,512]{1,0:T(8,128)(2,1)S(1)}, bf16[32,512]{1,0:T(8,128)(2,1)S(1)}, u32[]{:S(2)}, u32[]{:S(2)}) %collective-permute-start) | collective-permute-done | bytes 32800 | tf_op jit(solution)/shard_map/ppermute | solution.py:223
  5.9 2.6 %collective-permute-done.1.from_left = bf16[32,512]{1,0:T(8,128)(2,1)S(1)} collective-permute-done((bf16[32,512]{1,0:T(8,128)(2,1)S(1)}, bf16[32,512]{1,0:T(8,128)(2,1)S(1)}, u32[]{:S(2)}, u32[]{:S(2)}) %collective-permute-start.1) | collective-permute-done | bytes 32800 | tf_op jit(solution)/shard_map/ppermute | solution.py:223
  8.6 1.6 %collective-permute-start.2 = (bf16[32,512]{1,0:T(8,128)(2,1)S(1)}, bf16[32,512]{1,0:T(8,128)(2,1)S(1)}, u32[]{:S(2)}, u32[]{:S(2)}) collective-permute-start(bf16[32,512]{1,0:T(8,128)(2,1)S(1)} %get-tuple-element.18), channel_id=1, source_target_pairs={{0,1},{1,2},{2,3},{3,0},{4,5},{5,6},{6,7},{7,4},{8,9},{9,10},{10,1... | collective-permute-start | bytes 98312 | tf_op jit(solution)/shard_map/ppermute | solution.py:223
  10.2 2.2 %collective-permute-start.3 = (bf16[32,512]{1,0:T(8,128)(2,1)S(1)}, bf16[32,512]{1,0:T(8,128)(2,1)S(1)}, u32[]{:S(2)}, u32[]{:S(2)}) collective-permute-start(bf16[32,512]{1,0:T(8,128)(2,1)S(1)} %get-tuple-element.19), channel_id=1, source_target_pairs={{0,3},{1,0},{2,1},{3,2},{4,7},{5,4},{6,5},{7,6},{8,11},{9,8},{10,9... | collective-permute-start | bytes 98312 | tf_op jit(solution)/shard_map/ppermute | solution.py:223
  12.4 0.0 copy-start.12
  12.4 1.2 %copy-done.12 = bf16[1,1,1024,512]{3,2,1,0:T(8,128)(2,1)S(1)} copy-done((bf16[1,1,1024,512]{3,2,1,0:T(8,128)(2,1)S(1)}, bf16[1,1,1024,512]{3,2,1,0:T(8,128)(2,1)}, u32[]{:S(2)}) %copy-start.12) | copy-done | bytes 1048600
  13.6 0.0 copy-start.13
  13.6 1.0 %copy-done.13 = bf16[512,512]{1,0:T(8,128)(2,1)S(1)} copy-done((bf16[512,512]{1,0:T(8,128)(2,1)S(1)}, bf16[512,512]{1,0:T(8,128)(2,1)}, u32[]{:S(2)}) %copy-start.13) | copy-done | bytes 524312
  14.7 0.0 copy-start.14
  14.7 0.7 %copy-done.14 = s32[1,1,2048]{2,1,0:T(1,128)S(1)} copy-done((s32[1,1,2048]{2,1,0:T(1,128)S(1)}, s32[1,1,2048]{2,1,0:T(1,128)}, u32[]{:S(2)}) %copy-start.14) | copy-done | bytes 8216
  15.4 0.0 copy-start.1
  15.4 0.0 copy-start.3
  15.4 0.0 copy-start.4
  15.4 0.0 copy-start.6
  15.4 0.0 copy-start.7
  15.4 0.0 copy-start.8
  15.4 0.0 copy-start.9
  15.4 3.1 %grid_term.1 = f32[2048,512]{1,0:T(8,128)S(1)} custom-call(s32[1,2048]{1,0:T(1,128)S(1)} %bitcast.21, bf16[1024,512]{1,0:T(8,128)(2,1)S(1)} %bitcast.20, bf16[512,512]{1,0:T(8,128)(2,1)S(1)} %copy-done.13), custom_call_target="tpu_custom_call" | custom-call | flops 6000000000 | tf_op jit(solution)/shard_map/grid_term/pallas_call | solution.py:211
  18.6 0.0 copy-start.2
  18.6 0.0 copy-start.5
  18.6 0.0 copy-start.10
  18.6 0.0 copy-start.11
  18.6 0.0 collective-permute-done.2.from_below
  18.6 0.0 collective-permute-done.3.from_above
  18.6 0.0 copy-done.1
  18.6 0.0 copy-done.3
  18.6 0.0 copy-done.4
  18.7 0.0 copy-done.6
  18.7 0.0 copy-done.7
  18.7 0.0 copy-done.8
  18.7 0.0 copy-done.9
  18.7 3.3 %edge_sums.1 = (f32[160,512]{1,0:T(8,128)S(1)}, bf16[32,512]{1,0:T(8,128)(2,1)S(1)}, bf16[32,512]{1,0:T(8,128)(2,1)S(1)}, bf16[16,512]{1,0:T(8,128)(2,1)S(1)}, bf16[16,512]{1,0:T(8,128)(2,1)S(1)}) custom-call(f32[2048,512]{1,0:T(8,128)S(1)} %grid_term.1, bf16[160,512]{1,0:T(8,128)(2,1)S(1)} %bitcast.13, bf16[32,512]{1,0:T(8,128)(2,1)S(1)} %collective-permute-done.from_right, ...), custom_call_target="tpu_custom_call" | custom-call | tf_op jit(solution)/shard_map/edge_sums/pallas_call | solution.py:211
  22.0 0.1 collective-permute-start.4
  22.1 2.6 %collective-permute-start.5 = (bf16[32,512]{1,0:T(8,128)(2,1)S(1)}, bf16[32,512]{1,0:T(8,128)(2,1)S(1)}, u32[]{:S(2)}, u32[]{:S(2)}) collective-permute-start(bf16[32,512]{1,0:T(8,128)(2,1)S(1)} %get-tuple-element.22), channel_id=1, source_target_pairs={{0,28},{4,0},{8,4},{12,8},{16,12},{20,16},{24,20},{28,24},{1,29},{... | collective-permute-start | bytes 98312 | tf_op jit(solution)/shard_map/ppermute | solution.py:223
  24.7 1.6 %collective-permute-done.4.from_right.from_left = bf16[32,512]{1,0:T(8,128)(2,1)S(1)} collective-permute-done((bf16[32,512]{1,0:T(8,128)(2,1)S(1)}, bf16[32,512]{1,0:T(8,128)(2,1)S(1)}, u32[]{:S(2)}, u32[]{:S(2)}) %collective-permute-start.4) | collective-permute-done | bytes 32800 | tf_op jit(solution)/shard_map/ppermute | solution.py:223
  26.3 0.0 collective-permute-done.5.from_left.from_right
  26.3 0.1 collective-permute-start.6
  26.4 3.8 %collective-permute-start.7 = (bf16[32,512]{1,0:T(8,128)(2,1)S(1)}, bf16[32,512]{1,0:T(8,128)(2,1)S(1)}, u32[]{:S(2)}, u32[]{:S(2)}) collective-permute-start(bf16[32,512]{1,0:T(8,128)(2,1)S(1)} %get-tuple-element.26), channel_id=1, source_target_pairs={{0,3},{1,0},{2,1},{3,2},{4,7},{5,4},{6,5},{7,6},{8,11},{9,8},{10,9... | collective-permute-start | bytes 98312 | tf_op jit(solution)/shard_map/ppermute | solution.py:223
  30.2 1.9 %collective-permute-done.6.from_below = bf16[32,512]{1,0:T(8,128)(2,1)S(1)} collective-permute-done((bf16[32,512]{1,0:T(8,128)(2,1)S(1)}, bf16[32,512]{1,0:T(8,128)(2,1)S(1)}, u32[]{:S(2)}, u32[]{:S(2)}) %collective-permute-start.6) | collective-permute-done | bytes 32800 | tf_op jit(solution)/shard_map/ppermute | solution.py:223
  32.1 0.0 collective-permute-done.7.from_above
  32.1 0.0 copy-done.2
  32.1 0.0 copy-done.5
  32.1 0.0 copy-done.10
  32.1 0.0 copy-done.11
  32.1 0.7 %node_update.1 = bf16[160,512]{1,0:T(8,128)(2,1)S(1)} custom-call(bf16[160,512]{1,0:T(8,128)(2,1)S(1)} %bitcast.14, f32[160,512]{1,0:T(8,128)S(1)} %get-tuple-element.20.own_sum, bf16[32,512]{1,0:T(8,128)(2,1)S(1)} %collective-permute-done.4.from_right.from_left, bf16[32,512]{1,0:T(8,128)(2,1)S(1)} %collective-permute-done.5.from_left.from_right, ...), custom_call_target="tpu_custom_call" | custom-call | tf_op jit(solution)/shard_map/node_update/pallas_call | solution.py:211
  32.8 0.7 %copy.15 = bf16[1,1,160,512]{3,2,1,0:T(8,128)(2,1)} copy(bf16[1,1,160,512]{3,2,1,0:T(8,128)(2,1)S(1)} %bitcast.9) | data formatting | bytes 327680
  (3 shorter events, 0.0 us)
Async XLA Ops:
  0.0 0.9 %copy-start = (bf16[1,1,160,512]{3,2,1,0:T(8,128)(2,1)S(1)}, bf16[1,1,160,512]{3,2,1,0:T(8,128)(2,1)}, u32[]{:S(2)}) copy-start(bf16[1,1,160,512]{3,2,1,0:T(8,128)(2,1)} %param.15) | copy-start | bytes 491524
  0.9 5.0 %collective-permute-start = (bf16[32,512]{1,0:T(8,128)(2,1)S(1)}, bf16[32,512]{1,0:T(8,128)(2,1)S(1)}, u32[]{:S(2)}, u32[]{:S(2)}) collective-permute-start(bf16[32,512]{1,0:T(8,128)(2,1)S(1)} %get-tuple-element.16), channel_id=1, source_target_pairs={{0,28},{4,0},{8,4},{12,8},{16,12},{20,16},{24,20},{28,24},{1,29},{... | collective-permute-start | bytes 98312 | tf_op jit(solution)/shard_map/ppermute | solution.py:223
  4.3 4.2 %collective-permute-start.1 = (bf16[32,512]{1,0:T(8,128)(2,1)S(1)}, bf16[32,512]{1,0:T(8,128)(2,1)S(1)}, u32[]{:S(2)}, u32[]{:S(2)}) collective-permute-start(bf16[32,512]{1,0:T(8,128)(2,1)S(1)} %get-tuple-element.17), channel_id=1, source_target_pairs={{0,4},{4,8},{8,12},{12,16},{16,20},{20,24},{24,28},{28,0},{1,5},{5... | collective-permute-start | bytes 98312 | tf_op jit(solution)/shard_map/ppermute | solution.py:223
  8.6 10.0 %collective-permute-start.2 = (bf16[32,512]{1,0:T(8,128)(2,1)S(1)}, bf16[32,512]{1,0:T(8,128)(2,1)S(1)}, u32[]{:S(2)}, u32[]{:S(2)}) collective-permute-start(bf16[32,512]{1,0:T(8,128)(2,1)S(1)} %get-tuple-element.18), channel_id=1, source_target_pairs={{0,1},{1,2},{2,3},{3,0},{4,5},{5,6},{6,7},{7,4},{8,9},{9,10},{10,1... | collective-permute-start | bytes 98312 | tf_op jit(solution)/shard_map/ppermute | solution.py:223
  10.2 8.4 %collective-permute-start.3 = (bf16[32,512]{1,0:T(8,128)(2,1)S(1)}, bf16[32,512]{1,0:T(8,128)(2,1)S(1)}, u32[]{:S(2)}, u32[]{:S(2)}) collective-permute-start(bf16[32,512]{1,0:T(8,128)(2,1)S(1)} %get-tuple-element.19), channel_id=1, source_target_pairs={{0,3},{1,0},{2,1},{3,2},{4,7},{5,4},{6,5},{7,6},{8,11},{9,8},{10,9... | collective-permute-start | bytes 98312 | tf_op jit(solution)/shard_map/ppermute | solution.py:223
  12.4 1.2 %copy-start.12 = (bf16[1,1,1024,512]{3,2,1,0:T(8,128)(2,1)S(1)}, bf16[1,1,1024,512]{3,2,1,0:T(8,128)(2,1)}, u32[]{:S(2)}) copy-start(bf16[1,1,1024,512]{3,2,1,0:T(8,128)(2,1)} %param.14) | copy-start | bytes 3145732
  13.6 1.0 %copy-start.13 = (bf16[512,512]{1,0:T(8,128)(2,1)S(1)}, bf16[512,512]{1,0:T(8,128)(2,1)}, u32[]{:S(2)}) copy-start(bf16[512,512]{1,0:T(8,128)(2,1)} %w_grid.1) | copy-start | bytes 1572868
  14.7 0.7 %copy-start.14 = (s32[1,1,2048]{2,1,0:T(1,128)S(1)}, s32[1,1,2048]{2,1,0:T(1,128)}, u32[]{:S(2)}) copy-start(s32[1,1,2048]{2,1,0:T(1,128)} %param.17) | copy-start | bytes 24580
  15.4 3.2 %copy-start.1 = (bf16[1,1,160,512]{3,2,1,0:T(8,128)(2,1)S(1)}, bf16[1,1,160,512]{3,2,1,0:T(8,128)(2,1)}, u32[]{:S(2)}) copy-start(bf16[1,1,160,512]{3,2,1,0:T(8,128)(2,1)} %param.15) | copy-start | bytes 491524
  15.4 3.3 %copy-start.3 = (bf16[512,512]{1,0:T(8,128)(2,1)S(1)}, bf16[512,512]{1,0:T(8,128)(2,1)}, u32[]{:S(2)}) copy-start(bf16[512,512]{1,0:T(8,128)(2,1)} %w_mesh.1) | copy-start | bytes 1572868
  15.4 3.3 %copy-start.4 = (bf16[512,512]{1,0:T(8,128)(2,1)S(1)}, bf16[512,512]{1,0:T(8,128)(2,1)}, u32[]{:S(2)}) copy-start(bf16[512,512]{1,0:T(8,128)(2,1)} %w_message.1) | copy-start | bytes 1572868
  15.4 3.3 %copy-start.6 = (f32[1,1,4,2048]{3,2,1,0:T(4,128)S(1)}, f32[1,1,4,2048]{3,2,1,0:T(4,128)}, u32[]{:S(2)}) copy-start(f32[1,1,4,2048]{3,2,1,0:T(4,128)} %param.16) | copy-start | bytes 98308
  15.4 3.3 %copy-start.7 = (s32[1,1,2048]{2,1,0:T(1,128)S(1)}, s32[1,1,2048]{2,1,0:T(1,128)}, u32[]{:S(2)}) copy-start(s32[1,1,2048]{2,1,0:T(1,128)} %param.18) | copy-start | bytes 24580
  15.4 3.3 %copy-start.8 = (f32[4,512]{1,0:T(4,128)S(1)}, f32[4,512]{1,0:T(4,128)}, u32[]{:S(2)}) copy-start(f32[4,512]{1,0:T(4,128)} %w_edge.1) | copy-start | bytes 24580
  15.4 3.3 %copy-start.9 = (f32[512]{0:T(512)S(1)}, f32[512]{0:T(512)}, u32[]{:S(2)}) copy-start(f32[512]{0:T(512)} %param.22) | copy-start | bytes 6148
  18.6 13.5 %copy-start.2 = (bf16[1024,512]{1,0:T(8,128)(2,1)S(1)}, bf16[1024,512]{1,0:T(8,128)(2,1)}, u32[]{:S(2)}) copy-start(bf16[1024,512]{1,0:T(8,128)(2,1)} %w_node.1) | copy-start | bytes 3145732
  18.6 13.5 %copy-start.5 = (bf16[512,512]{1,0:T(8,128)(2,1)S(1)}, bf16[512,512]{1,0:T(8,128)(2,1)}, u32[]{:S(2)}) copy-start(bf16[512,512]{1,0:T(8,128)(2,1)} %w_output.1) | copy-start | bytes 1572868
  18.6 13.5 %copy-start.10 = (f32[512]{0:T(512)S(1)}, f32[512]{0:T(512)}, u32[]{:S(2)}) copy-start(f32[512]{0:T(512)} %param.26) | copy-start | bytes 6148
  18.6 13.5 %copy-start.11 = (f32[512]{0:T(512)S(1)}, f32[512]{0:T(512)}, u32[]{:S(2)}) copy-start(f32[512]{0:T(512)} %param.27) | copy-start | bytes 6148
  22.0 4.3 %collective-permute-start.4 = (bf16[32,512]{1,0:T(8,128)(2,1)S(1)}, bf16[32,512]{1,0:T(8,128)(2,1)S(1)}, u32[]{:S(2)}, u32[]{:S(2)}) collective-permute-start(bf16[32,512]{1,0:T(8,128)(2,1)S(1)} %get-tuple-element.21), channel_id=1, source_target_pairs={{0,4},{4,8},{8,12},{12,16},{16,20},{20,24},{24,28},{28,0},{1,5},{5... | collective-permute-start | bytes 98312 | tf_op jit(solution)/shard_map/ppermute | solution.py:223
  22.1 4.2 %collective-permute-start.5 = (bf16[32,512]{1,0:T(8,128)(2,1)S(1)}, bf16[32,512]{1,0:T(8,128)(2,1)S(1)}, u32[]{:S(2)}, u32[]{:S(2)}) collective-permute-start(bf16[32,512]{1,0:T(8,128)(2,1)S(1)} %get-tuple-element.22), channel_id=1, source_target_pairs={{0,28},{4,0},{8,4},{12,8},{16,12},{20,16},{24,20},{28,24},{1,29},{... | collective-permute-start | bytes 98312 | tf_op jit(solution)/shard_map/ppermute | solution.py:223
  26.3 5.8 %collective-permute-start.6 = (bf16[32,512]{1,0:T(8,128)(2,1)S(1)}, bf16[32,512]{1,0:T(8,128)(2,1)S(1)}, u32[]{:S(2)}, u32[]{:S(2)}) collective-permute-start(bf16[32,512]{1,0:T(8,128)(2,1)S(1)} %get-tuple-element.25), channel_id=1, source_target_pairs={{0,1},{1,2},{2,3},{3,0},{4,5},{5,6},{6,7},{7,4},{8,9},{9,10},{10,1... | collective-permute-start | bytes 98312 | tf_op jit(solution)/shard_map/ppermute | solution.py:223
  26.4 5.7 %collective-permute-start.7 = (bf16[32,512]{1,0:T(8,128)(2,1)S(1)}, bf16[32,512]{1,0:T(8,128)(2,1)S(1)}, u32[]{:S(2)}, u32[]{:S(2)}) collective-permute-start(bf16[32,512]{1,0:T(8,128)(2,1)S(1)} %get-tuple-element.26), channel_id=1, source_target_pairs={{0,3},{1,0},{2,1},{3,2},{4,7},{5,4},{6,5},{7,6},{8,11},{9,8},{10,9... | collective-permute-start | bytes 98312 | tf_op jit(solution)/shard_map/ppermute | solution.py:223

commit v3 on v2

--- a/solution.py
+++ b/solution.py
@@ -33,11 +33,16 @@
     return lax.dot_general(a, b, dims, preferred_element_type=f32)
 
 
-def grid_kernel(senders, grid_rows, w_grid, out, proj, *, block):
-    nodes = grid_rows.shape[0]
+def first_grid_kernel(senders, grid_rows, w_grid, packed, out, proj, *, block):
+    del packed
     proj[...] = dot(grid_rows[...], w_grid[...]).astype(bf16)
+    grid_kernel(senders, proj, out, block=block, offset=0)
+
+
+def grid_kernel(senders, proj, out, *, block, offset):
+    nodes = proj.shape[0]
     for start in range(0, out.shape[0], block):
-        picks = jnp.broadcast_to(senders[:, start : start + block], (128, block)).T
+        picks = jnp.broadcast_to(senders[:, offset + start : offset + start + block], (128, block)).T
         lane = lax.broadcasted_iota(jnp.int32, (block, 128), 1)
         onehot = jnp.concatenate(
             [(picks - base == lane).astype(f32).astype(bf16) for base in range(0, nodes, 128)],
@@ -47,7 +52,8 @@
 
 
 def edge_kernel(
-    grid_term,
+    grid_first,
+    grid_second,
     own_mesh,
     from_right,
     from_left,
@@ -117,13 +123,16 @@
     index = named - shift
 
     total = None
-    for start in range(0, grid_term.shape[0], block):
+    split = grid_first.shape[0]
+    for start in range(0, targets.shape[1], block):
+        grid_term = grid_first if start < split else grid_second
+        row = start if start < split else start - split
         ids = lax.broadcasted_iota(jnp.int32, (border_end, block), 0)
         onehot = (ids == index[:, start : start + block]).astype(f32).astype(bf16)
         picks = jnp.concatenate(
             [onehot, factors[:, start : start + block].astype(bf16)], axis=0
         )
-        preact = grid_term[start : start + block] + dot(
+        preact = grid_term[row : row + block] + dot(
             picks, table_bf16, (((0,), (0,)), ((), ()))
         )
         hidden = silu(preact).astype(bf16)
@@ -178,25 +187,39 @@
     out[...] = (own_mesh[...].astype(f32) + normed).astype(bf16)
 
 
-def pack_sides_kernel(own_mesh, to_left, to_right):
-    for out, slots in ((to_left, (5, 2, 8)), (to_right, (3, 0, 6))):
-        pieces = [
-            own_mesh[strip_row(slot) : strip_row(slot) + (B_SIDE if slot % 2 else CORNER_ROWS)]
-            for slot in slots
-        ]
-        out[...] = jnp.concatenate(pieces, axis=0)
+def pack_sides_kernel(own_mesh, to_left, to_right, low_side, high_side, sems):
+    copies = []
+    for out, slots in (
+        (to_left, (5, 2, 8)),
+        (to_right, (3, 0, 6)),
+        (low_side, (1,)),
+        (high_side, (7,)),
+    ):
+        place = 0
+        for slot in slots:
+            rows = B_SIDE if slot % 2 else CORNER_ROWS
+            copies.append(
+                pltpu.make_async_copy(
+                    own_mesh.at[pl.ds(strip_row(slot), rows)],
+                    out.at[pl.ds(place, rows)],
+                    sems.at[len(copies)],
+                )
+            )
+            place += rows
+    for copy in copies:
+        copy.start()
+    for copy in copies:
+        copy.wait()
 
 
 def pack_bands_kernel(
-    up_side, down_side, from_right, from_left, to_above, to_below, *, up_row, down_row, up_first
+    up_side, down_side, from_right, from_left, *rest, up_first
 ):
+    to_above, to_below = rest[-2:]
     first, second = B_SIDE, B_SIDE + CORNER_ROWS
     up, down = (first, second) if up_first else (second, first)
-    for out, side, row, corner in (
-        (to_above, up_side, up_row, up),
-        (to_below, down_side, down_row, down),
-    ):
-        out[:B_SIDE] = side[row : row + B_SIDE]
+    for out, side, corner in ((to_above, up_side, up), (to_below, down_side, down)):
+        out[:B_SIDE] = side[...]
         for i, ref in enumerate((from_right, from_left)):
             place = B_SIDE + i * CORNER_ROWS
             out[place : place + CORNER_ROWS] = ref[corner : corner + CORNER_ROWS]
@@ -206,11 +229,14 @@
     return pltpu.with_memory_space_constraint(x, pltpu.VMEM)
 
 
-def call(kernel, name, outs, args, scratch=(), flops=0):
+def call(kernel, name, outs, args, scratch=(), flops=0, on_vmem=True):
     cost = pl.CostEstimate(flops=flops, transcendentals=0, bytes_accessed=0) if flops else None
     return pl.pallas_call(
         kernel,
-        out_shape=tuple(pltpu.VMEM(shape, dtype) for shape, dtype in outs),
+        out_shape=tuple(
+            pltpu.VMEM(shape, dtype) if on_vmem else jax.ShapeDtypeStruct(shape, dtype)
+            for shape, dtype in outs
+        ),
         scratch_shapes=list(scratch),
         cost_estimate=cost,
         compiler_params=pltpu.CompilerParams(vmem_limit_bytes=24 * 2**20),
@@ -243,40 +269,53 @@
     own_mesh = mesh_latent[0, 0]
     mesh_rows, features = own_mesh.shape
     edges = senders.shape[2]
-    block = min(512, edges)
+    block = min(512, edges // 2)
     table_rows = mesh_rows + BORDER + GEOMETRY_ROWS
 
     packed = ((SEND_ROWS, features), bf16)
     strip = ((B_SIDE, features), bf16)
 
-    to_left, to_right = call(pack_sides_kernel, "pack_sides", (packed, packed), (own_mesh,))
+    to_left, to_right, low_side, high_side = pl.pallas_call(
+        pack_sides_kernel,
+        in_specs=[pl.BlockSpec(memory_space=pl.ANY)],
+        out_shape=tuple(pltpu.VMEM(shape, dtype) for shape, dtype in (packed, packed, strip, strip)),
+        scratch_shapes=[pltpu.SemaphoreType.DMA((8,))],
+        cost_estimate=pl.CostEstimate(flops=6_000_000_000, transcendentals=0, bytes_accessed=0),
+        compiler_params=pltpu.CompilerParams(vmem_limit_bytes=24 * 2**20),
+        name="pack_sides",
+    )(pltpu.with_memory_space_constraint(own_mesh, pltpu.HBM))
     from_right = shift_by(to_left, "lon", -1)
     from_left = shift_by(to_right, "lon", 1)
+    first_edges = max(edges // 2, 1)
+    grid_first, proj = call(
+        functools.partial(first_grid_kernel, block=min(block, first_edges)),
+        "grid_first",
+        (((first_edges, features), f32), (grid_rows.shape, bf16)),
+        (senders[0], grid_rows, w_grid, to_left),
+        flops=3_000_000_000,
+    )
     to_above, to_below = call(
-        functools.partial(
-            pack_bands_kernel, up_row=strip_row(1), down_row=strip_row(7), up_first=True
-        ),
+        functools.partial(pack_bands_kernel, up_first=True),
         "pack_bands",
         (packed, packed),
-        (own_mesh, own_mesh, from_right, from_left),
+        (low_side, high_side, from_right, from_left, grid_first),
     )
     from_below = shift_by(to_above, "lat", 1)
     from_above = shift_by(to_below, "lat", -1)
-
-    (grid_term,) = call(
-        functools.partial(grid_kernel, block=block),
-        "grid_term",
-        (((edges, features), f32),),
-        (senders[0], grid_rows, w_grid),
-        [pltpu.VMEM(grid_rows.shape, bf16)],
-        flops=6_000_000_000,
+    (grid_second,) = call(
+        functools.partial(grid_kernel, block=block, offset=first_edges),
+        "grid_second",
+        (((edges - first_edges, features), f32),),
+        (senders[0], proj),
+        flops=3_000_000_000,
     )
     own_sum, to_right, to_left, to_above, to_below = call(
         functools.partial(edge_kernel, block=block),
         "edge_sums",
         ((own_mesh.shape, f32), packed, packed, strip, strip),
         (
-            grid_term,
+            grid_first,
+            grid_second,
             own_mesh,
             from_right,
             from_left,
@@ -299,7 +338,7 @@
     got_left = shift_by(to_right, "lon", 1)
     got_right = shift_by(to_left, "lon", -1)
     to_above, to_below = call(
-        functools.partial(pack_bands_kernel, up_row=0, down_row=0, up_first=False),
+        functools.partial(pack_bands_kernel, up_first=False),
         "pack_sums",
         (packed, packed),
         (to_above, to_below, got_left, got_right),
@@ -323,6 +362,7 @@
             norm_bias[None],
         ),
         [pltpu.VMEM((mesh_rows, features), f32)],
+        on_vmem=False,
     )
     return mesh_out[None, None]
 

time: 33.8 us -> 29.7 us (0.88)
  local copies, waits for them, and re-layouts: 4.6 us -> 0.07 us
  Pallas kernels: 7.18 us -> 8.9 us
  waiting for transfers between devices: 7.73 us -> 6.53 us
    unnamed x31 -> x28, local copies, waits for them, and re-layouts: 4.6 us -> 0.07 us
    pallas_call x6 -> x7, Pallas kernels: 7.18 us -> 8.9 us  [the longest x6 7.91 us: call(): pl.pallas_call(kernel, out_shape=tuple((pltpu.VMEM(shape, dtype) if on_vm...]
    ppermute x8, waiting for transfers between devices: 7.73 us -> 6.53 us  [shift_by(): lax.ppermute(block, axis, [(i, (i + step) % count) for i in range(count)])]
  transfers between devices with their start and end apart: 8 -> 8, of which waited for: 4 -> 4; matrix products, arithmetic and copies ran while one was open for 0% -> 0% of each run, Pallas kernels for 9% -> 11%
where the time goes in v3:
time: 29.7 us; the launch traced here: 29.5 us
  starting transfers between devices  13.8 us (46%)
  Pallas kernels  8.9 us (30%)
  waiting for transfers between devices  6.53 us (22%)
    ppermute x8, starting transfers between devices, shift_by(): lax.ppermute(block, axis, [(i, (i + step) % count) for i in range(count)])  13.8 us
    pallas_call x6, Pallas kernels, call(): pl.pallas_call(kernel, out_shape=tuple((pltpu.VMEM(shape, dtype) if on_vm...  7.91 us
    ppermute x8, waiting for transfers between devices, shift_by(): lax.ppermute(block, axis, [(i, (i + step) % count) for i in range(count)])  6.53 us
    pallas_call x1, Pallas kernels, local(): pl.pallas_call(pack_sides_kernel, in_specs=[pl.BlockSpec(memory_space=pl....  0.99 us
  transfers between devices with their start and end apart: 8, of which 4 were waited for; matrix products, arithmetic and copies ran while one was open for 0% of the time, Pallas kernels for 11%

profile of v3, /device:TPU:0, one launch (start us, length us, event | category | flops | bytes accessed | tf_op | source)
XLA Modules:
  0.0 29.5 jit_solution(2676416831390736549)
XLA Ops:
  0.0 0.0 copy-start.11
  0.0 0.0 copy-start.12
  0.0 0.0 copy-start.13
  0.0 1.0 %pack_sides.1 = (bf16[32,512]{1,0:T(8,128)(2,1)S(1)}, bf16[32,512]{1,0:T(8,128)(2,1)S(1)}, bf16[16,512]{1,0:T(8,128)(2,1)S(1)}, bf16[16,512]{1,0:T(8,128)(2,1)S(1)}) custom-call(bf16[160,512]{1,0:T(8,128)(2,1)} %bitcast.9), custom_call_target="tpu_custom_call" | custom-call | flops 6000000000 | tf_op jit(solution)/shard_map/pack_sides/pallas_call | solution.py:278
  1.0 3.4 %collective-permute-start = (bf16[32,512]{1,0:T(8,128)(2,1)S(1)}, bf16[32,512]{1,0:T(8,128)(2,1)S(1)}, u32[]{:S(2)}, u32[]{:S(2)}) collective-permute-start(bf16[32,512]{1,0:T(8,128)(2,1)S(1)} %get-tuple-element.20.packed), channel_id=1, source_target_pairs={{0,28},{4,0},{8,4},{12,8},{16,12},{20,16},{24,20},{28,24},{1,29},{... | collective-permute-start | bytes 98312 | tf_op jit(solution)/shard_map/ppermute | solution.py:249
  4.4 0.0 collective-permute-start.1
  4.4 0.0 copy-done.11
  4.4 0.0 copy-done.12
  4.4 0.0 copy-done.13
  4.4 1.9 %grid_first.1 = (f32[1024,512]{1,0:T(8,128)S(1)}, bf16[1024,512]{1,0:T(8,128)(2,1)S(1)}) custom-call(s32[1,2048]{1,0:T(1,128)S(1)} %bitcast.18, bf16[1024,512]{1,0:T(8,128)(2,1)S(1)} %bitcast.17, bf16[512,512]{1,0:T(8,128)(2,1)S(1)} %copy-done.12, bf16[32,512]{1,0:T(8,128)(2,1)S(1)} %get-tuple-element.20.packed), custom_call_target="tpu_custom_call" | custom-call | flops 3000000000 | tf_op jit(solution)/shard_map/grid_first/pallas_call | solution.py:234
  6.3 0.0 collective-permute-done.from_right
  6.3 2.3 %collective-permute-done.1.from_left = bf16[32,512]{1,0:T(8,128)(2,1)S(1)} collective-permute-done((bf16[32,512]{1,0:T(8,128)(2,1)S(1)}, bf16[32,512]{1,0:T(8,128)(2,1)S(1)}, u32[]{:S(2)}, u32[]{:S(2)}) %collective-permute-start.1) | collective-permute-done | bytes 32800 | tf_op jit(solution)/shard_map/ppermute | solution.py:249
  8.7 1.6 %collective-permute-start.2 = (bf16[32,512]{1,0:T(8,128)(2,1)S(1)}, bf16[32,512]{1,0:T(8,128)(2,1)S(1)}, u32[]{:S(2)}, u32[]{:S(2)}) collective-permute-start(bf16[32,512]{1,0:T(8,128)(2,1)S(1)} %get-tuple-element.26), channel_id=1, source_target_pairs={{0,1},{1,2},{2,3},{3,0},{4,5},{5,6},{6,7},{7,4},{8,9},{9,10},{10,1... | collective-permute-start | bytes 98312 | tf_op jit(solution)/shard_map/ppermute | solution.py:249
  10.2 2.2 %collective-permute-start.3 = (bf16[32,512]{1,0:T(8,128)(2,1)S(1)}, bf16[32,512]{1,0:T(8,128)(2,1)S(1)}, u32[]{:S(2)}, u32[]{:S(2)}) collective-permute-start(bf16[32,512]{1,0:T(8,128)(2,1)S(1)} %get-tuple-element.27), channel_id=1, source_target_pairs={{0,3},{1,0},{2,1},{3,2},{4,7},{5,4},{6,5},{7,6},{8,11},{9,8},{10,9... | collective-permute-start | bytes 98312 | tf_op jit(solution)/shard_map/ppermute | solution.py:249
  12.5 0.0 copy-start.1
  12.5 0.0 copy-start.2
  12.5 0.0 copy-start.3
  12.5 0.0 copy-start.5
  12.5 0.0 copy-start.6
  12.5 0.0 copy-start.7
  12.5 0.0 copy-start.8
  12.5 1.3 %grid_second.1 = f32[1024,512]{1,0:T(8,128)S(1)} custom-call(s32[1,2048]{1,0:T(1,128)S(1)} %bitcast.19, bf16[1024,512]{1,0:T(8,128)(2,1)S(1)} %get-tuple-element.22.proj), custom_call_target="tpu_custom_call" | custom-call | flops 3000000000 | tf_op jit(solution)/shard_map/grid_second/pallas_call | solution.py:234
  13.8 0.6 %collective-permute-done.2.from_below = bf16[32,512]{1,0:T(8,128)(2,1)S(1)} collective-permute-done((bf16[32,512]{1,0:T(8,128)(2,1)S(1)}, bf16[32,512]{1,0:T(8,128)(2,1)S(1)}, u32[]{:S(2)}, u32[]{:S(2)}) %collective-permute-start.2) | collective-permute-done | bytes 32800 | tf_op jit(solution)/shard_map/ppermute | solution.py:249
  14.5 0.0 collective-permute-done.3.from_above
  14.5 0.0 copy-done.1
  14.5 0.0 copy-done.2
  14.5 0.0 copy-done.3
  14.5 0.0 copy-done.5
  14.5 0.0 copy-done.6
  14.5 0.0 copy-done.7
  14.6 0.0 copy-done.8
  14.6 0.0 copy-start
  14.6 0.0 copy-start.4
  14.6 0.0 copy-start.9
  14.6 0.0 copy-start.10
  14.6 3.3 %edge_sums.1 = (f32[160,512]{1,0:T(8,128)S(1)}, bf16[32,512]{1,0:T(8,128)(2,1)S(1)}, bf16[32,512]{1,0:T(8,128)(2,1)S(1)}, bf16[16,512]{1,0:T(8,128)(2,1)S(1)}, bf16[16,512]{1,0:T(8,128)(2,1)S(1)}) custom-call(f32[1024,512]{1,0:T(8,128)S(1)} %get-tuple-element.21.rest_0_.grid_first, f32[1024,512]{1,0:T(8,128)S(1)} %grid_second.1, ...), custom_call_target="tpu_custom_call" | custom-call | tf_op jit(solution)/shard_map/edge_sums/pallas_call | solution.py:234
  17.9 0.1 collective-permute-start.4
  18.0 2.6 %collective-permute-start.5 = (bf16[32,512]{1,0:T(8,128)(2,1)S(1)}, bf16[32,512]{1,0:T(8,128)(2,1)S(1)}, u32[]{:S(2)}, u32[]{:S(2)}) collective-permute-start(bf16[32,512]{1,0:T(8,128)(2,1)S(1)} %get-tuple-element.30), channel_id=1, source_target_pairs={{0,28},{4,0},{8,4},{12,8},{16,12},{20,16},{24,20},{28,24},{1,29},{... | collective-permute-start | bytes 98312 | tf_op jit(solution)/shard_map/ppermute | solution.py:249
  20.6 1.6 %collective-permute-done.4.from_right.from_left = bf16[32,512]{1,0:T(8,128)(2,1)S(1)} collective-permute-done((bf16[32,512]{1,0:T(8,128)(2,1)S(1)}, bf16[32,512]{1,0:T(8,128)(2,1)S(1)}, u32[]{:S(2)}, u32[]{:S(2)}) %collective-permute-start.4) | collective-permute-done | bytes 32800 | tf_op jit(solution)/shard_map/ppermute | solution.py:249
  22.3 0.0 collective-permute-done.5.from_left.from_right
  22.3 1.2 %collective-permute-start.6 = (bf16[32,512]{1,0:T(8,128)(2,1)S(1)}, bf16[32,512]{1,0:T(8,128)(2,1)S(1)}, u32[]{:S(2)}, u32[]{:S(2)}) collective-permute-start(bf16[32,512]{1,0:T(8,128)(2,1)S(1)} %get-tuple-element.33), channel_id=1, source_target_pairs={{0,1},{1,2},{2,3},{3,0},{4,5},{5,6},{6,7},{7,4},{8,9},{9,10},{10,1... | collective-permute-start | bytes 98312 | tf_op jit(solution)/shard_map/ppermute | solution.py:249
  23.5 2.7 %collective-permute-start.7 = (bf16[32,512]{1,0:T(8,128)(2,1)S(1)}, bf16[32,512]{1,0:T(8,128)(2,1)S(1)}, u32[]{:S(2)}, u32[]{:S(2)}) collective-permute-start(bf16[32,512]{1,0:T(8,128)(2,1)S(1)} %get-tuple-element.34), channel_id=1, source_target_pairs={{0,3},{1,0},{2,1},{3,2},{4,7},{5,4},{6,5},{7,6},{8,11},{9,8},{10,9... | collective-permute-start | bytes 98312 | tf_op jit(solution)/shard_map/ppermute | solution.py:249
  26.1 1.9 %collective-permute-done.6.from_below = bf16[32,512]{1,0:T(8,128)(2,1)S(1)} collective-permute-done((bf16[32,512]{1,0:T(8,128)(2,1)S(1)}, bf16[32,512]{1,0:T(8,128)(2,1)S(1)}, u32[]{:S(2)}, u32[]{:S(2)}) %collective-permute-start.6) | collective-permute-done | bytes 32800 | tf_op jit(solution)/shard_map/ppermute | solution.py:249
  28.0 0.0 collective-permute-done.7.from_above
  28.0 0.0 copy-done
  28.0 0.0 copy-done.4
  28.0 0.0 copy-done.9
  28.0 0.0 copy-done.10
  28.1 1.4 %node_update.1 = bf16[160,512]{1,0:T(8,128)(2,1)} custom-call(bf16[160,512]{1,0:T(8,128)(2,1)S(1)} %bitcast.11, f32[160,512]{1,0:T(8,128)S(1)} %get-tuple-element.28.own_sum, bf16[32,512]{1,0:T(8,128)(2,1)S(1)} %collective-permute-done.4.from_right.from_left, bf16[32,512]{1,0:T(8,128)(2,1)S(1)} %collective-permute-done.5.from_left.from_right, ...), custom_call_target="tpu_custom_call" | custom-call | tf_op jit(solution)/shard_map/node_update/pallas_call | solution.py:234
  (2 shorter events, 0.0 us)
Async XLA Ops:
  0.0 4.4 %copy-start.11 = (bf16[1,1,1024,512]{3,2,1,0:T(8,128)(2,1)S(1)}, bf16[1,1,1024,512]{3,2,1,0:T(8,128)(2,1)}, u32[]{:S(2)}) copy-start(bf16[1,1,1024,512]{3,2,1,0:T(8,128)(2,1)} %param.14) | copy-start | bytes 3145732
  0.0 4.4 %copy-start.12 = (bf16[512,512]{1,0:T(8,128)(2,1)S(1)}, bf16[512,512]{1,0:T(8,128)(2,1)}, u32[]{:S(2)}) copy-start(bf16[512,512]{1,0:T(8,128)(2,1)} %w_grid.1) | copy-start | bytes 1572868
  0.0 4.4 %copy-start.13 = (s32[1,1,2048]{2,1,0:T(1,128)S(1)}, s32[1,1,2048]{2,1,0:T(1,128)}, u32[]{:S(2)}) copy-start(s32[1,1,2048]{2,1,0:T(1,128)} %param.17) | copy-start | bytes 24580
  1.0 5.3 %collective-permute-start = (bf16[32,512]{1,0:T(8,128)(2,1)S(1)}, bf16[32,512]{1,0:T(8,128)(2,1)S(1)}, u32[]{:S(2)}, u32[]{:S(2)}) collective-permute-start(bf16[32,512]{1,0:T(8,128)(2,1)S(1)} %get-tuple-element.20.packed), channel_id=1, source_target_pairs={{0,28},{4,0},{8,4},{12,8},{16,12},{20,16},{24,20},{28,24},{1,29},{... | collective-permute-start | bytes 98312 | tf_op jit(solution)/shard_map/ppermute | solution.py:249
  4.4 4.2 %collective-permute-start.1 = (bf16[32,512]{1,0:T(8,128)(2,1)S(1)}, bf16[32,512]{1,0:T(8,128)(2,1)S(1)}, u32[]{:S(2)}, u32[]{:S(2)}) collective-permute-start(bf16[32,512]{1,0:T(8,128)(2,1)S(1)} %get-tuple-element.23), channel_id=1, source_target_pairs={{0,4},{4,8},{8,12},{12,16},{16,20},{20,24},{24,28},{28,0},{1,5},{5... | collective-permute-start | bytes 98312 | tf_op jit(solution)/shard_map/ppermute | solution.py:249
  8.7 5.8 %collective-permute-start.2 = (bf16[32,512]{1,0:T(8,128)(2,1)S(1)}, bf16[32,512]{1,0:T(8,128)(2,1)S(1)}, u32[]{:S(2)}, u32[]{:S(2)}) collective-permute-start(bf16[32,512]{1,0:T(8,128)(2,1)S(1)} %get-tuple-element.26), channel_id=1, source_target_pairs={{0,1},{1,2},{2,3},{3,0},{4,5},{5,6},{6,7},{7,4},{8,9},{9,10},{10,1... | collective-permute-start | bytes 98312 | tf_op jit(solution)/shard_map/ppermute | solution.py:249
  10.2 4.3 %collective-permute-start.3 = (bf16[32,512]{1,0:T(8,128)(2,1)S(1)}, bf16[32,512]{1,0:T(8,128)(2,1)S(1)}, u32[]{:S(2)}, u32[]{:S(2)}) collective-permute-start(bf16[32,512]{1,0:T(8,128)(2,1)S(1)} %get-tuple-element.27), channel_id=1, source_target_pairs={{0,3},{1,0},{2,1},{3,2},{4,7},{5,4},{6,5},{7,6},{8,11},{9,8},{10,9... | collective-permute-start | bytes 98312 | tf_op jit(solution)/shard_map/ppermute | solution.py:249
  12.5 2.0 %copy-start.1 = (bf16[1,1,160,512]{3,2,1,0:T(8,128)(2,1)S(1)}, bf16[1,1,160,512]{3,2,1,0:T(8,128)(2,1)}, u32[]{:S(2)}) copy-start(bf16[1,1,160,512]{3,2,1,0:T(8,128)(2,1)} %param.15) | copy-start | bytes 491524
  12.5 2.0 %copy-start.2 = (bf16[512,512]{1,0:T(8,128)(2,1)S(1)}, bf16[512,512]{1,0:T(8,128)(2,1)}, u32[]{:S(2)}) copy-start(bf16[512,512]{1,0:T(8,128)(2,1)} %w_mesh.1) | copy-start | bytes 1572868
  12.5 2.0 %copy-start.3 = (bf16[512,512]{1,0:T(8,128)(2,1)S(1)}, bf16[512,512]{1,0:T(8,128)(2,1)}, u32[]{:S(2)}) copy-start(bf16[512,512]{1,0:T(8,128)(2,1)} %w_message.1) | copy-start | bytes 1572868
  12.5 2.0 %copy-start.5 = (f32[1,1,4,2048]{3,2,1,0:T(4,128)S(1)}, f32[1,1,4,2048]{3,2,1,0:T(4,128)}, u32[]{:S(2)}) copy-start(f32[1,1,4,2048]{3,2,1,0:T(4,128)} %param.16) | copy-start | bytes 98308
  12.5 2.0 %copy-start.6 = (s32[1,1,2048]{2,1,0:T(1,128)S(1)}, s32[1,1,2048]{2,1,0:T(1,128)}, u32[]{:S(2)}) copy-start(s32[1,1,2048]{2,1,0:T(1,128)} %param.18) | copy-start | bytes 24580
  12.5 2.0 %copy-start.7 = (f32[4,512]{1,0:T(4,128)S(1)}, f32[4,512]{1,0:T(4,128)}, u32[]{:S(2)}) copy-start(f32[4,512]{1,0:T(4,128)} %w_edge.1) | copy-start | bytes 24580
  12.5 2.0 %copy-start.8 = (f32[512]{0:T(512)S(1)}, f32[512]{0:T(512)}, u32[]{:S(2)}) copy-start(f32[512]{0:T(512)} %param.22) | copy-start | bytes 6148
  14.6 13.5 %copy-start = (bf16[1024,512]{1,0:T(8,128)(2,1)S(1)}, bf16[1024,512]{1,0:T(8,128)(2,1)}, u32[]{:S(2)}) copy-start(bf16[1024,512]{1,0:T(8,128)(2,1)} %w_node.1) | copy-start | bytes 3145732
  14.6 13.5 %copy-start.4 = (bf16[512,512]{1,0:T(8,128)(2,1)S(1)}, bf16[512,512]{1,0:T(8,128)(2,1)}, u32[]{:S(2)}) copy-start(bf16[512,512]{1,0:T(8,128)(2,1)} %w_output.1) | copy-start | bytes 1572868
  14.6 13.5 %copy-start.9 = (f32[512]{0:T(512)S(1)}, f32[512]{0:T(512)}, u32[]{:S(2)}) copy-start(f32[512]{0:T(512)} %param.26) | copy-start | bytes 6148
  14.6 13.4 %copy-start.10 = (f32[512]{0:T(512)S(1)}, f32[512]{0:T(512)}, u32[]{:S(2)}) copy-start(f32[512]{0:T(512)} %param.27) | copy-start | bytes 6148
  17.9 4.3 %collective-permute-start.4 = (bf16[32,512]{1,0:T(8,128)(2,1)S(1)}, bf16[32,512]{1,0:T(8,128)(2,1)S(1)}, u32[]{:S(2)}, u32[]{:S(2)}) collective-permute-start(bf16[32,512]{1,0:T(8,128)(2,1)S(1)} %get-tuple-element.29), channel_id=1, source_target_pairs={{0,4},{4,8},{8,12},{12,16},{16,20},{20,24},{24,28},{28,0},{1,5},{5... | collective-permute-start | bytes 98312 | tf_op jit(solution)/shard_map/ppermute | solution.py:249
  18.0 4.3 %collective-permute-start.5 = (bf16[32,512]{1,0:T(8,128)(2,1)S(1)}, bf16[32,512]{1,0:T(8,128)(2,1)S(1)}, u32[]{:S(2)}, u32[]{:S(2)}) collective-permute-start(bf16[32,512]{1,0:T(8,128)(2,1)S(1)} %get-tuple-element.30), channel_id=1, source_target_pairs={{0,28},{4,0},{8,4},{12,8},{16,12},{20,16},{24,20},{28,24},{1,29},{... | collective-permute-start | bytes 98312 | tf_op jit(solution)/shard_map/ppermute | solution.py:249
  22.3 5.8 %collective-permute-start.6 = (bf16[32,512]{1,0:T(8,128)(2,1)S(1)}, bf16[32,512]{1,0:T(8,128)(2,1)S(1)}, u32[]{:S(2)}, u32[]{:S(2)}) collective-permute-start(bf16[32,512]{1,0:T(8,128)(2,1)S(1)} %get-tuple-element.33), channel_id=1, source_target_pairs={{0,1},{1,2},{2,3},{3,0},{4,5},{5,6},{6,7},{7,4},{8,9},{9,10},{10,1... | collective-permute-start | bytes 98312 | tf_op jit(solution)/shard_map/ppermute | solution.py:249
  23.5 4.5 %collective-permute-start.7 = (bf16[32,512]{1,0:T(8,128)(2,1)S(1)}, bf16[32,512]{1,0:T(8,128)(2,1)S(1)}, u32[]{:S(2)}, u32[]{:S(2)}) collective-permute-start(bf16[32,512]{1,0:T(8,128)(2,1)S(1)} %get-tuple-element.34), channel_id=1, source_target_pairs={{0,3},{1,0},{2,1},{3,2},{4,7},{5,4},{6,5},{7,6},{8,11},{9,8},{10,9... | collective-permute-start | bytes 98312 | tf_op jit(solution)/shard_map/ppermute | solution.py:249

commit v4 on v3

--- a/solution.py
+++ b/solution.py
@@ -22,6 +22,12 @@
 
 def strip_row(slot):
     return (slot if slot < 4 else slot - 1) * B_SIDE
+
+
+def partner_row(even_slot, odd_slot):
+    odd = lax.axis_index("lon") % 2
+    low, high = strip_row(even_slot), strip_row(odd_slot)
+    return pl.multiple_of(low + odd * (high - low), CORNER_ROWS)
 
 
 def silu(x):
@@ -55,8 +61,8 @@
     grid_first,
     grid_second,
     own_mesh,
-    from_right,
-    from_left,
+    from_first,
+    from_second,
     from_below,
     from_above,
     targets,
@@ -78,7 +84,7 @@
 ):
     mesh_rows = own_mesh.shape[0]
     border_end = mesh_rows + BORDER
-    received = (from_right, from_left, from_below, from_above)
+    received = (from_first, from_second, from_below, from_above)
     table[:mesh_rows] = dot(own_mesh[...], w_mesh[...])
     arrived = dot(jnp.concatenate([ref[...] for ref in received], axis=0), w_mesh[...])
     row = mesh_rows
@@ -114,11 +120,13 @@
     for i, slot in enumerate(corner_slots):
         places[slot] = mesh_rows + len(side_slots) * B_SIDE + i * B_CORNER
     named = targets[...]
+    odd = lax.axis_index("lon") % 2
     shift = jnp.zeros_like(named)
     for slot in range(9):
         base = slot * mesh_rows
         if slot != 4:
-            base += strip_row(slot) - places[slot]
+            mirrored = slot // 3 * 3 + 2 - slot % 3
+            base += strip_row(slot) - places[slot] + odd * (places[slot] - places[mirrored])
         shift = jnp.where(named >= slot * mesh_rows, base, shift)
     index = named - shift
 
@@ -157,8 +165,8 @@
 def node_kernel(
     own_mesh,
     own_sum,
-    from_left,
-    from_right,
+    from_first,
+    from_second,
     from_below,
     from_above,
     w_node,
@@ -170,12 +178,16 @@
 ):
     features = own_mesh.shape[1]
     agg[...] = own_sum[...]
-    for ref, slots in ((from_left, (5,)), (from_right, (3,)), (from_below, (7, 8, 6)), (from_above, (1, 2, 0))):
+    for ref, places in (
+        (from_first, (partner_row(3, 5),)),
+        (from_second, (partner_row(5, 3),)),
+        (from_below, (strip_row(7), partner_row(6, 8), partner_row(8, 6))),
+        (from_above, (strip_row(1), partner_row(0, 2), partner_row(2, 0))),
+    ):
         first = 0
-        for slot in slots:
-            rows = B_SIDE if slot % 2 else CORNER_ROWS
-            place = strip_row(slot)
-            agg[place : place + rows] += ref[...].astype(f32)[first : first + rows]
+        for i, place in enumerate(places):
+            rows = CORNER_ROWS if i else B_SIDE
+            agg[pl.ds(place, rows)] += ref[...].astype(f32)[first : first + rows]
             first += rows
     hidden = dot(own_mesh[...], w_node[:features]) + dot(agg[...].astype(bf16), w_node[features:])
     hidden = silu(hidden).astype(bf16)
@@ -187,20 +199,21 @@
     out[...] = (own_mesh[...].astype(f32) + normed).astype(bf16)
 
 
-def pack_sides_kernel(own_mesh, to_left, to_right, low_side, high_side, sems):
+def pack_sides_kernel(own_mesh, to_first, to_second, low_side, high_side, sems):
+    rows_of = (
+        (to_first, [partner_row(3, 5), partner_row(0, 2), partner_row(6, 8)]),
+        (to_second, [partner_row(5, 3), partner_row(2, 0), partner_row(8, 6)]),
+        (low_side, [strip_row(1)]),
+        (high_side, [strip_row(7)]),
+    )
     copies = []
-    for out, slots in (
-        (to_left, (5, 2, 8)),
-        (to_right, (3, 0, 6)),
-        (low_side, (1,)),
-        (high_side, (7,)),
-    ):
+    for out, sources in rows_of:
         place = 0
-        for slot in slots:
-            rows = B_SIDE if slot % 2 else CORNER_ROWS
+        for i, source in enumerate(sources):
+            rows = CORNER_ROWS if i else B_SIDE
             copies.append(
                 pltpu.make_async_copy(
-                    own_mesh.at[pl.ds(strip_row(slot), rows)],
+                    own_mesh.at[pl.ds(source, rows)],
                     out.at[pl.ds(place, rows)],
                     sems.at[len(copies)],
                 )
@@ -213,14 +226,14 @@
 
 
 def pack_bands_kernel(
-    up_side, down_side, from_right, from_left, *rest, up_first
+    up_side, down_side, from_first, from_second, *rest, up_first
 ):
     to_above, to_below = rest[-2:]
     first, second = B_SIDE, B_SIDE + CORNER_ROWS
     up, down = (first, second) if up_first else (second, first)
     for out, side, corner in ((to_above, up_side, up), (to_below, down_side, down)):
         out[:B_SIDE] = side[...]
-        for i, ref in enumerate((from_right, from_left)):
+        for i, ref in enumerate((from_first, from_second)):
             place = B_SIDE + i * CORNER_ROWS
             out[place : place + CORNER_ROWS] = ref[corner : corner + CORNER_ROWS]
 
@@ -247,6 +260,14 @@
 def shift_by(block, axis, step):
     count = lax.axis_size(axis)
     return lax.ppermute(block, axis, [(i, (i + step) % count) for i in range(count)])
+
+
+def swap(block, axis, start):
+    count = lax.axis_size(axis)
+    pairs = []
+    for i in range(start, count, 2):
+        pairs += [(i, (i + 1) % count), ((i + 1) % count, i)]
+    return lax.ppermute(block, axis, pairs)
 
 
 def local(
@@ -284,8 +305,8 @@
         compiler_params=pltpu.CompilerParams(vmem_limit_bytes=24 * 2**20),
         name="pack_sides",
     )(pltpu.with_memory_space_constraint(own_mesh, pltpu.HBM))
-    from_right = shift_by(to_left, "lon", -1)
-    from_left = shift_by(to_right, "lon", 1)
+    from_first = swap(to_left, "lon", 0)
+    from_second = swap(to_right, "lon", 1)
     first_edges = max(edges // 2, 1)
     grid_first, proj = call(
         functools.partial(first_grid_kernel, block=min(block, first_edges)),
@@ -298,7 +319,7 @@
         functools.partial(pack_bands_kernel, up_first=True),
         "pack_bands",
         (packed, packed),
-        (low_side, high_side, from_right, from_left, grid_first),
+        (low_side, high_side, from_first, from_second, grid_first),
     )
     from_below = shift_by(to_above, "lat", 1)
     from_above = shift_by(to_below, "lat", -1)
@@ -317,8 +338,8 @@
             grid_first,
             grid_second,
             own_mesh,
-            from_right,
-            from_left,
+            from_first,
+            from_second,
             from_below,
             from_above,
             receivers[0],
@@ -335,13 +356,13 @@
         ],
     )
 
-    got_left = shift_by(to_right, "lon", 1)
-    got_right = shift_by(to_left, "lon", -1)
+    got_first = swap(to_right, "lon", 0)
+    got_second = swap(to_left, "lon", 1)
     to_above, to_below = call(
         functools.partial(pack_bands_kernel, up_first=False),
         "pack_sums",
         (packed, packed),
-        (to_above, to_below, got_left, got_right),
+        (to_above, to_below, got_first, got_second),
     )
     got_below = shift_by(to_above, "lat", 1)
     got_above = shift_by(to_below, "lat", -1)
@@ -352,8 +373,8 @@
         (
             own_mesh,
             own_sum,
-            got_left,
-            got_right,
+            got_first,
+            got_second,
             got_below,
             got_above,
             w_node,

time: 29.7 us -> 28.3 us (0.953)
  waiting for transfers between devices: 6.53 us -> 4.97 us
    ppermute x0 -> x4, starting transfers between devices: none -> 6.16 us  [swap(): return lax.ppermute(block, axis, pairs)]
    ppermute x8 -> x4, starting transfers between devices: 13.8 us -> 7.7 us  [shift_by(): lax.ppermute(block, axis, [(i, (i + step) % count) for i in range(count)])]
    ppermute x8 -> x4, waiting for transfers between devices: 6.53 us -> 2.63 us  [shift_by(): lax.ppermute(block, axis, [(i, (i + step) % count) for i in range(count)])]
    ppermute x0 -> x4, waiting for transfers between devices: none -> 2.34 us  [swap(): return lax.ppermute(block, axis, pairs)]
  transfers between devices with their start and end apart: 8 -> 8, of which waited for: 4 -> 3; matrix products, arithmetic and copies ran while one was open for 0% -> 0% of each run, Pallas kernels for 11% -> 11%
where the time goes in v4:
time: 28.3 us; the launch traced here: 28 us
  starting transfers between devices  13.9 us (49%)
  Pallas kernels  8.94 us (32%)
  waiting for transfers between devices  4.97 us (18%)
    pallas_call x6, Pallas kernels, call(): pl.pallas_call(kernel, out_shape=tuple((pltpu.VMEM(shape, dtype) if on_vm...  7.95 us
    ppermute x4, starting transfers between devices, shift_by(): lax.ppermute(block, axis, [(i, (i + step) % count) for i in range(count)])  7.7 us
    ppermute x4, starting transfers between devices, swap(): return lax.ppermute(block, axis, pairs)  6.16 us
    ppermute x4, waiting for transfers between devices, shift_by(): lax.ppermute(block, axis, [(i, (i + step) % count) for i in range(count)])  2.63 us
    ppermute x4, waiting for transfers between devices, swap(): return lax.ppermute(block, axis, pairs)  2.34 us
    pallas_call x1, Pallas kernels, local(): pl.pallas_call(pack_sides_kernel, in_specs=[pl.BlockSpec(memory_space=pl....  0.99 us
  transfers between devices with their start and end apart: 8, of which 3 were waited for; matrix products, arithmetic and copies ran while one was open for 0% of the time, Pallas kernels for 11%

profile of v4, /device:TPU:0, one launch (start us, length us, event | category | flops | bytes accessed | tf_op | source)
XLA Modules:
  0.0 28.0 jit_solution(14227804699471610473)
XLA Ops:
  0.0 0.0 copy-start.11
  0.0 0.0 copy-start.12
  0.0 0.0 copy-start.13
  0.0 1.0 %pack_sides.1 = (bf16[32,512]{1,0:T(8,128)(2,1)S(1)}, bf16[32,512]{1,0:T(8,128)(2,1)S(1)}, bf16[16,512]{1,0:T(8,128)(2,1)S(1)}, bf16[16,512]{1,0:T(8,128)(2,1)S(1)}) custom-call(bf16[160,512]{1,0:T(8,128)(2,1)} %bitcast.9), custom_call_target="tpu_custom_call" | custom-call | flops 6000000000 | tf_op jit(solution)/shard_map/pack_sides/pallas_call | solution.py:299
  1.0 0.6 %collective-permute-start = (bf16[32,512]{1,0:T(8,128)(2,1)S(1)}, bf16[32,512]{1,0:T(8,128)(2,1)S(1)}, u32[]{:S(2)}, u32[]{:S(2)}) collective-permute-start(bf16[32,512]{1,0:T(8,128)(2,1)S(1)} %get-tuple-element.20.packed), channel_id=1, source_target_pairs={{0,4},{4,0},{8,12},{12,8},{16,20},{20,16},{24,28},{28,24},{1,5},{5... | collective-permute-start | bytes 98312 | tf_op jit(solution)/shard_map/ppermute | solution.py:270
  1.6 3.5 %collective-permute-start.1 = (bf16[32,512]{1,0:T(8,128)(2,1)S(1)}, bf16[32,512]{1,0:T(8,128)(2,1)S(1)}, u32[]{:S(2)}, u32[]{:S(2)}) collective-permute-start(bf16[32,512]{1,0:T(8,128)(2,1)S(1)} %get-tuple-element.23), channel_id=1, source_target_pairs={{4,8},{8,4},{12,16},{16,12},{20,24},{24,20},{28,0},{0,28},{5,9},{9... | collective-permute-start | bytes 98312 | tf_op jit(solution)/shard_map/ppermute | solution.py:270
  5.1 0.0 copy-done.11
  5.1 0.0 copy-done.12
  5.1 0.0 copy-done.13
  5.1 1.9 %grid_first.1 = (f32[1024,512]{1,0:T(8,128)S(1)}, bf16[1024,512]{1,0:T(8,128)(2,1)S(1)}) custom-call(s32[1,2048]{1,0:T(1,128)S(1)} %bitcast.18, bf16[1024,512]{1,0:T(8,128)(2,1)S(1)} %bitcast.17, bf16[512,512]{1,0:T(8,128)(2,1)S(1)} %copy-done.12, bf16[32,512]{1,0:T(8,128)(2,1)S(1)} %get-tuple-element.20.packed), custom_call_target="tpu_custom_call" | custom-call | flops 3000000000 | tf_op jit(solution)/shard_map/grid_first/pallas_call | solution.py:247
  7.0 0.0 collective-permute-done.from_first
  7.0 0.0 collective-permute-done.1.from_second
  7.1 1.6 %collective-permute-start.2 = (bf16[32,512]{1,0:T(8,128)(2,1)S(1)}, bf16[32,512]{1,0:T(8,128)(2,1)S(1)}, u32[]{:S(2)}, u32[]{:S(2)}) collective-permute-start(bf16[32,512]{1,0:T(8,128)(2,1)S(1)} %get-tuple-element.26), channel_id=1, source_target_pairs={{0,1},{1,2},{2,3},{3,0},{4,5},{5,6},{6,7},{7,4},{8,9},{9,10},{10,1... | collective-permute-start | bytes 98312 | tf_op jit(solution)/shard_map/ppermute | solution.py:262
  8.7 2.3 %collective-permute-start.3 = (bf16[32,512]{1,0:T(8,128)(2,1)S(1)}, bf16[32,512]{1,0:T(8,128)(2,1)S(1)}, u32[]{:S(2)}, u32[]{:S(2)}) collective-permute-start(bf16[32,512]{1,0:T(8,128)(2,1)S(1)} %get-tuple-element.27), channel_id=1, source_target_pairs={{0,3},{1,0},{2,1},{3,2},{4,7},{5,4},{6,5},{7,6},{8,11},{9,8},{10,9... | collective-permute-start | bytes 98312 | tf_op jit(solution)/shard_map/ppermute | solution.py:262
  10.9 0.0 copy-start.1
  10.9 0.0 copy-start.2
  10.9 0.0 copy-start.3
  10.9 0.0 copy-start.5
  11.0 0.0 copy-start.6
  11.0 0.0 copy-start.7
  11.0 0.0 copy-start.8
  11.0 1.3 %grid_second.1 = f32[1024,512]{1,0:T(8,128)S(1)} custom-call(s32[1,2048]{1,0:T(1,128)S(1)} %bitcast.19, bf16[1024,512]{1,0:T(8,128)(2,1)S(1)} %get-tuple-element.22.proj), custom_call_target="tpu_custom_call" | custom-call | flops 3000000000 | tf_op jit(solution)/shard_map/grid_second/pallas_call | solution.py:247
  12.3 0.7 %collective-permute-done.2.from_below = bf16[32,512]{1,0:T(8,128)(2,1)S(1)} collective-permute-done((bf16[32,512]{1,0:T(8,128)(2,1)S(1)}, bf16[32,512]{1,0:T(8,128)(2,1)S(1)}, u32[]{:S(2)}, u32[]{:S(2)}) %collective-permute-start.2) | collective-permute-done | bytes 32800 | tf_op jit(solution)/shard_map/ppermute | solution.py:262
  13.0 0.0 collective-permute-done.3.from_above
  13.0 0.0 copy-done.1
  13.0 0.0 copy-done.2
  13.0 0.0 copy-done.3
  13.0 0.0 copy-done.5
  13.1 0.0 copy-done.6
  13.1 0.0 copy-done.7
  13.1 0.0 copy-done.8
  13.1 0.0 copy-start
  13.1 0.0 copy-start.4
  13.1 0.0 copy-start.9
  13.1 0.0 copy-start.10
  13.1 3.3 %edge_sums.1 = (f32[160,512]{1,0:T(8,128)S(1)}, bf16[32,512]{1,0:T(8,128)(2,1)S(1)}, bf16[32,512]{1,0:T(8,128)(2,1)S(1)}, bf16[16,512]{1,0:T(8,128)(2,1)S(1)}, bf16[16,512]{1,0:T(8,128)(2,1)S(1)}) custom-call(f32[1024,512]{1,0:T(8,128)S(1)} %get-tuple-element.21.rest_0_.grid_first, f32[1024,512]{1,0:T(8,128)S(1)} %grid_second.1, ...), custom_call_target="tpu_custom_call" | custom-call | tf_op jit(solution)/shard_map/edge_sums/pallas_call | solution.py:247
  16.4 0.1 collective-permute-start.4
  16.5 2.0 %collective-permute-start.5 = (bf16[32,512]{1,0:T(8,128)(2,1)S(1)}, bf16[32,512]{1,0:T(8,128)(2,1)S(1)}, u32[]{:S(2)}, u32[]{:S(2)}) collective-permute-start(bf16[32,512]{1,0:T(8,128)(2,1)S(1)} %get-tuple-element.30), channel_id=1, source_target_pairs={{4,8},{8,4},{12,16},{16,12},{20,24},{24,20},{28,0},{0,28},{5,9},{9... | collective-permute-start | bytes 98312 | tf_op jit(solution)/shard_map/ppermute | solution.py:270
  18.5 0.0 collective-permute-done.4.from_first
  18.5 2.3 %collective-permute-done.5.from_second = bf16[32,512]{1,0:T(8,128)(2,1)S(1)} collective-permute-done((bf16[32,512]{1,0:T(8,128)(2,1)S(1)}, bf16[32,512]{1,0:T(8,128)(2,1)S(1)}, u32[]{:S(2)}, u32[]{:S(2)}) %collective-permute-start.5) | collective-permute-done | bytes 32800 | tf_op jit(solution)/shard_map/ppermute | solution.py:270
  20.8 1.1 %collective-permute-start.6 = (bf16[32,512]{1,0:T(8,128)(2,1)S(1)}, bf16[32,512]{1,0:T(8,128)(2,1)S(1)}, u32[]{:S(2)}, u32[]{:S(2)}) collective-permute-start(bf16[32,512]{1,0:T(8,128)(2,1)S(1)} %get-tuple-element.33), channel_id=1, source_target_pairs={{0,1},{1,2},{2,3},{3,0},{4,5},{5,6},{6,7},{7,4},{8,9},{9,10},{10,1... | collective-permute-start | bytes 98312 | tf_op jit(solution)/shard_map/ppermute | solution.py:262
  22.0 2.7 %collective-permute-start.7 = (bf16[32,512]{1,0:T(8,128)(2,1)S(1)}, bf16[32,512]{1,0:T(8,128)(2,1)S(1)}, u32[]{:S(2)}, u32[]{:S(2)}) collective-permute-start(bf16[32,512]{1,0:T(8,128)(2,1)S(1)} %get-tuple-element.34), channel_id=1, source_target_pairs={{0,3},{1,0},{2,1},{3,2},{4,7},{5,4},{6,5},{7,6},{8,11},{9,8},{10,9... | collective-permute-start | bytes 98312 | tf_op jit(solution)/shard_map/ppermute | solution.py:262
  24.6 1.9 %collective-permute-done.6.from_below = bf16[32,512]{1,0:T(8,128)(2,1)S(1)} collective-permute-done((bf16[32,512]{1,0:T(8,128)(2,1)S(1)}, bf16[32,512]{1,0:T(8,128)(2,1)S(1)}, u32[]{:S(2)}, u32[]{:S(2)}) %collective-permute-start.6) | collective-permute-done | bytes 32800 | tf_op jit(solution)/shard_map/ppermute | solution.py:262
  26.5 0.0 collective-permute-done.7.from_above
  26.5 0.0 copy-done
  26.5 0.0 copy-done.4
  26.5 0.0 copy-done.9
  26.6 0.0 copy-done.10
  26.6 1.5 %node_update.1 = bf16[160,512]{1,0:T(8,128)(2,1)} custom-call(bf16[160,512]{1,0:T(8,128)(2,1)S(1)} %bitcast.11, f32[160,512]{1,0:T(8,128)S(1)} %get-tuple-element.28.own_sum, bf16[32,512]{1,0:T(8,128)(2,1)S(1)} %collective-permute-done.4.from_first, bf16[32,512]{1,0:T(8,128)(2,1)S(1)} %collective-permute-done.5.from_second, ...), custom_call_target="tpu_custom_call" | custom-call | tf_op jit(solution)/shard_map/node_update/pallas_call | solution.py:247
  (2 shorter events, 0.0 us)
Async XLA Ops:
  0.0 5.1 %copy-start.11 = (bf16[1,1,1024,512]{3,2,1,0:T(8,128)(2,1)S(1)}, bf16[1,1,1024,512]{3,2,1,0:T(8,128)(2,1)}, u32[]{:S(2)}) copy-start(bf16[1,1,1024,512]{3,2,1,0:T(8,128)(2,1)} %param.14) | copy-start | bytes 3145732
  0.0 5.1 %copy-start.12 = (bf16[512,512]{1,0:T(8,128)(2,1)S(1)}, bf16[512,512]{1,0:T(8,128)(2,1)}, u32[]{:S(2)}) copy-start(bf16[512,512]{1,0:T(8,128)(2,1)} %w_grid.1) | copy-start | bytes 1572868
  0.0 5.1 %copy-start.13 = (s32[1,1,2048]{2,1,0:T(1,128)S(1)}, s32[1,1,2048]{2,1,0:T(1,128)}, u32[]{:S(2)}) copy-start(s32[1,1,2048]{2,1,0:T(1,128)} %param.17) | copy-start | bytes 24580
  1.0 6.0 %collective-permute-start = (bf16[32,512]{1,0:T(8,128)(2,1)S(1)}, bf16[32,512]{1,0:T(8,128)(2,1)S(1)}, u32[]{:S(2)}, u32[]{:S(2)}) collective-permute-start(bf16[32,512]{1,0:T(8,128)(2,1)S(1)} %get-tuple-element.20.packed), channel_id=1, source_target_pairs={{0,4},{4,0},{8,12},{12,8},{16,20},{20,16},{24,28},{28,24},{1,5},{5... | collective-permute-start | bytes 98312 | tf_op jit(solution)/shard_map/ppermute | solution.py:270
  1.6 5.5 %collective-permute-start.1 = (bf16[32,512]{1,0:T(8,128)(2,1)S(1)}, bf16[32,512]{1,0:T(8,128)(2,1)S(1)}, u32[]{:S(2)}, u32[]{:S(2)}) collective-permute-start(bf16[32,512]{1,0:T(8,128)(2,1)S(1)} %get-tuple-element.23), channel_id=1, source_target_pairs={{4,8},{8,4},{12,16},{16,12},{20,24},{24,20},{28,0},{0,28},{5,9},{9... | collective-permute-start | bytes 98312 | tf_op jit(solution)/shard_map/ppermute | solution.py:270
  7.1 6.0 %collective-permute-start.2 = (bf16[32,512]{1,0:T(8,128)(2,1)S(1)}, bf16[32,512]{1,0:T(8,128)(2,1)S(1)}, u32[]{:S(2)}, u32[]{:S(2)}) collective-permute-start(bf16[32,512]{1,0:T(8,128)(2,1)S(1)} %get-tuple-element.26), channel_id=1, source_target_pairs={{0,1},{1,2},{2,3},{3,0},{4,5},{5,6},{6,7},{7,4},{8,9},{9,10},{10,1... | collective-permute-start | bytes 98312 | tf_op jit(solution)/shard_map/ppermute | solution.py:262
  8.7 4.3 %collective-permute-start.3 = (bf16[32,512]{1,0:T(8,128)(2,1)S(1)}, bf16[32,512]{1,0:T(8,128)(2,1)S(1)}, u32[]{:S(2)}, u32[]{:S(2)}) collective-permute-start(bf16[32,512]{1,0:T(8,128)(2,1)S(1)} %get-tuple-element.27), channel_id=1, source_target_pairs={{0,3},{1,0},{2,1},{3,2},{4,7},{5,4},{6,5},{7,6},{8,11},{9,8},{10,9... | collective-permute-start | bytes 98312 | tf_op jit(solution)/shard_map/ppermute | solution.py:262
  10.9 2.1 %copy-start.1 = (bf16[1,1,160,512]{3,2,1,0:T(8,128)(2,1)S(1)}, bf16[1,1,160,512]{3,2,1,0:T(8,128)(2,1)}, u32[]{:S(2)}) copy-start(bf16[1,1,160,512]{3,2,1,0:T(8,128)(2,1)} %param.15) | copy-start | bytes 491524
  10.9 2.1 %copy-start.2 = (bf16[512,512]{1,0:T(8,128)(2,1)S(1)}, bf16[512,512]{1,0:T(8,128)(2,1)}, u32[]{:S(2)}) copy-start(bf16[512,512]{1,0:T(8,128)(2,1)} %w_mesh.1) | copy-start | bytes 1572868
  10.9 2.1 %copy-start.3 = (bf16[512,512]{1,0:T(8,128)(2,1)S(1)}, bf16[512,512]{1,0:T(8,128)(2,1)}, u32[]{:S(2)}) copy-start(bf16[512,512]{1,0:T(8,128)(2,1)} %w_message.1) | copy-start | bytes 1572868
  10.9 2.1 %copy-start.5 = (f32[1,1,4,2048]{3,2,1,0:T(4,128)S(1)}, f32[1,1,4,2048]{3,2,1,0:T(4,128)}, u32[]{:S(2)}) copy-start(f32[1,1,4,2048]{3,2,1,0:T(4,128)} %param.16) | copy-start | bytes 98308
  11.0 2.1 %copy-start.6 = (s32[1,1,2048]{2,1,0:T(1,128)S(1)}, s32[1,1,2048]{2,1,0:T(1,128)}, u32[]{:S(2)}) copy-start(s32[1,1,2048]{2,1,0:T(1,128)} %param.18) | copy-start | bytes 24580
  11.0 2.1 %copy-start.7 = (f32[4,512]{1,0:T(4,128)S(1)}, f32[4,512]{1,0:T(4,128)}, u32[]{:S(2)}) copy-start(f32[4,512]{1,0:T(4,128)} %w_edge.1) | copy-start | bytes 24580
  11.0 2.1 %copy-start.8 = (f32[512]{0:T(512)S(1)}, f32[512]{0:T(512)}, u32[]{:S(2)}) copy-start(f32[512]{0:T(512)} %param.22) | copy-start | bytes 6148
  13.1 13.5 %copy-start = (bf16[1024,512]{1,0:T(8,128)(2,1)S(1)}, bf16[1024,512]{1,0:T(8,128)(2,1)}, u32[]{:S(2)}) copy-start(bf16[1024,512]{1,0:T(8,128)(2,1)} %w_node.1) | copy-start | bytes 3145732
  13.1 13.4 %copy-start.4 = (bf16[512,512]{1,0:T(8,128)(2,1)S(1)}, bf16[512,512]{1,0:T(8,128)(2,1)}, u32[]{:S(2)}) copy-start(bf16[512,512]{1,0:T(8,128)(2,1)} %w_output.1) | copy-start | bytes 1572868
  13.1 13.4 %copy-start.9 = (f32[512]{0:T(512)S(1)}, f32[512]{0:T(512)}, u32[]{:S(2)}) copy-start(f32[512]{0:T(512)} %param.26) | copy-start | bytes 6148
  13.1 13.4 %copy-start.10 = (f32[512]{0:T(512)S(1)}, f32[512]{0:T(512)}, u32[]{:S(2)}) copy-start(f32[512]{0:T(512)} %param.27) | copy-start | bytes 6148
  16.4 2.1 %collective-permute-start.4 = (bf16[32,512]{1,0:T(8,128)(2,1)S(1)}, bf16[32,512]{1,0:T(8,128)(2,1)S(1)}, u32[]{:S(2)}, u32[]{:S(2)}) collective-permute-start(bf16[32,512]{1,0:T(8,128)(2,1)S(1)} %get-tuple-element.29), channel_id=1, source_target_pairs={{0,4},{4,0},{8,12},{12,8},{16,20},{20,16},{24,28},{28,24},{1,5},{5... | collective-permute-start | bytes 98312 | tf_op jit(solution)/shard_map/ppermute | solution.py:270
  16.5 4.3 %collective-permute-start.5 = (bf16[32,512]{1,0:T(8,128)(2,1)S(1)}, bf16[32,512]{1,0:T(8,128)(2,1)S(1)}, u32[]{:S(2)}, u32[]{:S(2)}) collective-permute-start(bf16[32,512]{1,0:T(8,128)(2,1)S(1)} %get-tuple-element.30), channel_id=1, source_target_pairs={{4,8},{8,4},{12,16},{16,12},{20,24},{24,20},{28,0},{0,28},{5,9},{9... | collective-permute-start | bytes 98312 | tf_op jit(solution)/shard_map/ppermute | solution.py:270
  20.8 5.7 %collective-permute-start.6 = (bf16[32,512]{1,0:T(8,128)(2,1)S(1)}, bf16[32,512]{1,0:T(8,128)(2,1)S(1)}, u32[]{:S(2)}, u32[]{:S(2)}) collective-permute-start(bf16[32,512]{1,0:T(8,128)(2,1)S(1)} %get-tuple-element.33), channel_id=1, source_target_pairs={{0,1},{1,2},{2,3},{3,0},{4,5},{5,6},{6,7},{7,4},{8,9},{9,10},{10,1... | collective-permute-start | bytes 98312 | tf_op jit(solution)/shard_map/ppermute | solution.py:262
  22.0 4.6 %collective-permute-start.7 = (bf16[32,512]{1,0:T(8,128)(2,1)S(1)}, bf16[32,512]{1,0:T(8,128)(2,1)S(1)}, u32[]{:S(2)}, u32[]{:S(2)}) collective-permute-start(bf16[32,512]{1,0:T(8,128)(2,1)S(1)} %get-tuple-element.34), channel_id=1, source_target_pairs={{0,3},{1,0},{2,1},{3,2},{4,7},{5,4},{6,5},{7,6},{8,11},{9,8},{10,9... | collective-permute-start | bytes 98312 | tf_op jit(solution)/shard_map/ppermute | solution.py:262
